TPU v7x, 128 devices: a whole 4x4x4 slice. The times are simulated.
128 devices in a mesh: gx: 8 (over y, z_hi), gy: 4 (over x), gz: 4 (over z_lo, core).
Axes of the slice: x: 4, y: 4, z: 4 (z_hi: 2, z_lo: 2; z = z_hi * 2 + z_lo), core: 2. Of those that a mesh axis runs over, the one named last changes fastest.
Arguments:
- log_range: float32 [256, 128, 512], P('gx', 'gy', 'gz'), may hold values from 0.7 to 2
- state: float32 [2, 256, 128, 512], P(None, 'gx', 'gy', 'gz'), may hold values from -60 to 60, as said below
- adjoint_start: float32 [2, 256, 128, 512], P(None, 'gx', 'gy', 'gz'), may hold values from -0.3 to 0.3
- obs_index: int32 [2, 8, 4, 4, 4096], P(None, 'gx', 'gy', 'gz'), may hold values from 0 to 131071
- obs_value: float32 [2, 8, 4, 4, 4096], P(None, 'gx', 'gy', 'gz'), may hold values from -6 to 6
Outputs:
- gradient: float32 [256, 128, 512], P('gx', 'gy', 'gz')
- adjoint: float32 [2, 256, 128, 512], P(None, 'gx', 'gy', 'gz')
Inputs may be any that keep to these rules, and one draw needn't show every extreme that they name: `obs_index`: each entry numbers a cell of its own device's block as (a * 32 + b) * 128 + c; cells may repeat. `state`: real values.
All inputs are finite; a program needn't handle non-finite values.
Results may differ from a plain program's by a relative error of at most 0.0001.
Values sent between devices are 32-bit elements; how exact they have to be, the bound alone decides.
A program may use at most 320 MiB of HBM per device.

v0:
```python
import jax
import jax.numpy as jnp
from jax import lax
from jax.sharding import Mesh
from jax.sharding import PartitionSpec as P

ITERS = 4
GX_GY_GZ = ("gx_0", "gx_1", "gy", "gz_0", "gz_1")
GX = ("gx_0", "gx_1")
GZ = ("gz_0", "gz_1")


noise_var = 0.25


def padded_2(shard, sides, width):
    edges = {}
    for axis, dim in sides:
        peers, length = (lax.axis_size(axis), shard.shape[dim])
        up = [(i, (i + 1) % peers) for i in range(peers)]
        last = lax.slice_in_dim(shard, length - width, length, axis=dim)
        leading = lax.slice_in_dim(shard, 0, width, axis=dim)
        edges[dim] = (
            lax.ppermute(last, axis, up),
            lax.ppermute(leading, axis, [(b, a) for a, b in up]),
        )
    done = []
    for _, dim in sides:
        low, high = edges[dim]
        around = [(width, width) if d in done else (0, 0) for d in range(shard.ndim)]
        shard = jnp.concatenate([jnp.pad(low, around), shard, jnp.pad(high, around)], axis=dim)
        done.append(dim)
    return shard


def one_axis_at_a_time(shard, axes):
    for axis in axes:
        shard = lax.psum(shard, axis)
    return shard


def stencil(padded, center, kappa_sq):
    beside = padded[:, 2:, 1:-1, 1:-1] + padded[:, :-2, 1:-1, 1:-1]
    beside = beside + padded[:, 1:-1, 2:, 1:-1] + padded[:, 1:-1, :-2, 1:-1]
    beside = beside + padded[:, 1:-1, 1:-1, 2:] + padded[:, 1:-1, 1:-1, :-2]
    return (kappa_sq[None] + 6.0) * center - beside


def one_pass(field, kappa_sq):
    padded = padded_2(field, ((GX, 1), ("gy", 2), (GZ, 3)), 1)
    return stencil(padded, field, kappa_sq)


def two_products(residual, image):
    return (
        one_axis_at_a_time(jnp.sum(residual * residual, axis=(1, 2, 3)), GX_GY_GZ),
        one_axis_at_a_time(jnp.sum(residual * image, axis=(1, 2, 3)), GX_GY_GZ),
    )


def widen(values):
    return values[:, None, None, None]


def on_device(log_range, state, adjoint_start, obs_index, obs_value):
    replicas = state.shape[0]
    field_shape = state.shape
    cells = field_shape[1] * field_shape[2] * field_shape[3]
    kappa_sq = 4.0 * jnp.exp(-2.0 * log_range)
    observed = obs_index.reshape(replicas, -1)
    measured = obs_value.reshape(replicas, -1)
    row_ids = jnp.arange(replicas, dtype=jnp.int32)[:, None]
    payload = jnp.stack([jnp.ones_like(measured), measured], 0)
    scattered = jnp.zeros((2, replicas, cells), jnp.float32).at[:, row_ids, observed].add(payload)
    counted = scattered[0].reshape(field_shape)
    value_sum = scattered[1].reshape(field_shape)
    obs_weight = counted / noise_var
    right_side = (value_sum - counted * state) / noise_var

    def first_image(stack):
        applied = one_pass(stack, kappa_sq)
        return (applied, applied)

    def second_image(inner):
        return one_pass(inner, kappa_sq)

    def system(vector):
        inner, applied = first_image(vector)
        return (second_image(inner) + obs_weight * vector, applied)

    adjoint = adjoint_start
    start_image, unused = system(adjoint)
    residual = right_side - start_image
    image, residual_image = system(residual)
    norm_now, product = two_products(residual, image)
    step_size = norm_now / product
    direction, along = (residual, image)
    direction_image = residual_image
    for iteration in range(ITERS):
        adjoint = adjoint + widen(step_size) * direction
        if iteration + 1 < ITERS:
            residual = residual - widen(step_size) * along
            image, residual_image = system(residual)
            norm_next, product = two_products(residual, image)
            ratio = norm_next / norm_now
            step_size = norm_next / (product - ratio * norm_next / step_size)
            direction = residual + widen(ratio) * direction
            direction_image = residual_image + widen(ratio) * direction_image
            along = image + widen(ratio) * along
            norm_now = norm_next
    joined = jnp.concatenate([state, adjoint], 0)
    padded = padded_2(joined, ((GX, 1), ("gy", 2), (GZ, 3)), 1)
    images = stencil(padded, joined, kappa_sq)
    state_image = images[:replicas]
    adjoint_image = images[replicas:]
    terms = -2.0 * kappa_sq[None] * (adjoint * state_image + adjoint_image * state)
    gradient = jnp.sum(terms, axis=0)
    return (gradient, adjoint)


def solution(mesh):
    split = Mesh(
        mesh.devices.reshape(4, 2, mesh.shape["gy"], 2, 2), ("gx_0", "gx_1", "gy", "gz_0", "gz_1")
    )
    in_specs = (
        P(GX, "gy", GZ),
        P(None, GX, "gy", GZ),
        P(None, GX, "gy", GZ),
        P(None, GX, "gy", GZ, None),
        P(None, GX, "gy", GZ, None),
    )
    out_specs = (P(GX, "gy", GZ), P(None, GX, "gy", GZ))
    return jax.shard_map(
        on_device, mesh=split, in_specs=in_specs, out_specs=out_specs, check_vma=False
    )
```

profile of v0, /device:TPU:1, one launch (start us, length us, event | category | flops | bytes accessed | tf_op | source)
XLA Modules:
  0.0 700.6 jit_solution(6151561714889434283)
XLA Ops:
  1.4 6.9 collective-permute-start
  17.1 5.9 sort
  23.1 13.9 %copy.8 = f32[8192,2]{1,0:T(8,128)} copy(f32[8192,2]{0,1:T(2,128)S(1)} %bitcast.17) | data formatting | bytes 131072 | tf_op jit(solution)/shard_map/stack | solution.py:73
  36.9 150.0 %scatter_custom_fusion = f32[2,262144]{0,1:T(8,128)} fusion(s32[8192]{0:T(1024)S(1)} %get-tuple-element.2, f32[]{:T(128)} %constant.10.clone.1, f32[8192,2]{1,0:T(8,128)} %copy.8, s32[8192]{0:T(1024)S(1)} %broadcast_clamp_fusion), kind=kCustom, calls=%fused_computation.4 | custom fusion | flops 16384 | bytes 2097664
  200.8 3.7 collective-permute-start.6
  210.4 128.4 %slice_reduce_fusion = (f32[262144]{0:T(1024)}, f32[262144]{0:T(1024)}) fusion(f32[2,262144]{0,1:T(8,128)} %scatter_custom_fusion), kind=kLoop, calls=%fused_computation.2 | loop fusion | bytes 4194304 | tf_op jit(solution)/shard_map/slice | solution.py:75
  341.8 6.4 fusion.94
  348.5 4.9 collective-permute-start.12
  353.4 2.8 collective-permute-start.14
  365.6 3.7 fusion.84
  369.5 5.1 collective-permute-start.18
  374.5 2.7 collective-permute-start.20
  388.5 6.9 multiply_reduce_fusion.5
  395.4 6.0 all-reduce.52
  401.4 5.3 all-reduce.64
  406.6 6.0 all-reduce.48
  412.6 3.9 all-reduce.60
  416.5 9.0 %all-reduce.56 = (f32[2]{0:T(128)S(1)}, f32[2]{0:T(128)S(1)}) all-reduce(f32[2]{0:T(128)S(1)} %get-tuple-element.42, f32[2]{0:T(128)S(1)} %get-tuple-element.43), channel_id=1, replica_groups=mesh['gx_0'=4,'gx_1'=2,'gy'=4,'gz_0'=2,'gz_1'=2] {'gz_1'}, use_global_device_ids=true, to_apply=%region_6.7 | all-reduce | flops 4 | bytes 32 | tf_op jit(solution)/shard_map/psum | solution.py:38
  427.5 4.8 collective-permute-start.24
  444.6 3.5 fusion.67
  448.3 5.1 collective-permute-start.30
  467.6 6.9 multiply_reduce_fusion.3
  474.5 6.0 all-reduce.51
  480.5 5.3 all-reduce.63
  485.7 6.0 all-reduce.47
  491.7 3.8 all-reduce.59
  495.5 9.0 %all-reduce.55 = (f32[2]{0:T(128)S(1)}, f32[2]{0:T(128)S(1)}) all-reduce(f32[2]{0:T(128)S(1)} %get-tuple-element.40, f32[2]{0:T(128)S(1)} %get-tuple-element.41), channel_id=1, replica_groups=mesh['gx_0'=4,'gx_1'=2,'gy'=4,'gz_0'=2,'gz_1'=2] {'gz_1'}, use_global_device_ids=true, to_apply=%region_18.19 | all-reduce | flops 4 | bytes 32 | tf_op jit(solution)/shard_map/psum | solution.py:38
  507.0 4.8 collective-permute-start.36
  525.1 3.7 fusion.50
  529.0 5.1 collective-permute-start.42
  547.9 7.4 %multiply_reduce_fusion.1 = (f32[2]{0:T(128)S(1)}, f32[2]{0:T(128)S(1)}, f32[2,32,32,128]{3,2,1,0:T(8,128)}) fusion(f32[2,32,32,128]{3,2,1,0:T(8,128)S(1)} %multiply_subtract_fusion.1, f32[2,32,32,128]{3,2,1,0:T(8,128)} %bitcast.12, f32[2,34,1,128]{3,2,1,0:T(1,128)S(1)} %pad.165, f32[2,1,32,128]{3,2,1,0:T(8,128)S(1)} %collective-permute-done.42, ...), kind=kLoop, calls=%fused_computation.327 | loop fusion | flops 9961468 | bytes 4870160 | tf_op jit(solution)/shard_map/reduce_sum | solution.py:57
  555.2 6.0 all-reduce.50
  561.2 5.3 all-reduce.62
  566.5 6.0 all-reduce.46
  572.5 3.9 all-reduce.58
  576.3 9.0 %all-reduce.54 = (f32[2]{0:T(128)S(1)}, f32[2]{0:T(128)S(1)}) all-reduce(f32[2]{0:T(128)S(1)} %get-tuple-element.38, f32[2]{0:T(128)S(1)} %get-tuple-element.39), channel_id=1, replica_groups=mesh['gx_0'=4,'gx_1'=2,'gy'=4,'gz_0'=2,'gz_1'=2] {'gz_1'}, use_global_device_ids=true, to_apply=%region_30.31 | all-reduce | flops 4 | bytes 32 | tf_op jit(solution)/shard_map/psum | solution.py:38
  588.1 4.8 collective-permute-start.48
  606.0 5.9 fusion.33
  612.0 5.1 collective-permute-start.54
  630.9 6.2 fusion.25
  637.1 6.0 all-reduce.49
  643.1 5.3 all-reduce.61
  648.4 6.0 all-reduce.45
  654.4 3.8 all-reduce.57
  658.2 9.0 %all-reduce.53 = (f32[2]{0:T(128)S(1)}, f32[2]{0:T(128)S(1)}) all-reduce(f32[2]{0:T(128)S(1)} %get-tuple-element.36, f32[2]{0:T(128)S(1)} %get-tuple-element.37), channel_id=1, replica_groups=mesh['gx_0'=4,'gx_1'=2,'gy'=4,'gz_0'=2,'gz_1'=2] {'gz_1'}, use_global_device_ids=true, to_apply=%region_42.43 | all-reduce | flops 4 | bytes 32 | tf_op jit(solution)/shard_map/psum | solution.py:38
  673.1 4.8 collective-permute-start.60
  677.9 2.8 fusion.6
  692.5 6.5 fusion.9
  (284 shorter events, 159.8 us)
Async XLA Ops:
  1.4 190.3 %collective-permute-start = (f32[2,1,32,128]{3,2,1,0:T(8,128)S(1)}, f32[2,1,32,128]{3,2,1,0:T(8,128)S(1)}, u32[]{:S(2)}, u32[]{:S(2)}) collective-permute-start(f32[2,1,32,128]{3,2,1,0:T(8,128)S(1)} %get-tuple-element.129), channel_id=1, source_target_pairs={{16,0},{32,16},{48,32},{64,48},{80,64},{96,80},{112,96},{0,112},{1... | collective-permute-start | bytes 98312 | tf_op jit(solution)/shard_map/ppermute | solution.py:25
  8.3 183.2 %collective-permute-start.1 = (f32[2,1,32,128]{3,2,1,0:T(8,128)S(1)}, f32[2,1,32,128]{3,2,1,0:T(8,128)S(1)}, u32[]{:S(2)}, u32[]{:S(2)}) collective-permute-start(f32[2,1,32,128]{3,2,1,0:T(8,128)S(1)} %get-tuple-element.130), channel_id=1, source_target_pairs={{0,16},{16,32},{32,48},{48,64},{64,80},{80,96},{96,112},{112,0},{1... | collective-permute-start | bytes 98312 | tf_op jit(solution)/shard_map/ppermute | solution.py:24
  9.4 182.2 %collective-permute-start.3 = (f32[2,32,1,128]{3,2,1,0:T(1,128)S(1)}, f32[2,32,1,128]{3,2,1,0:T(1,128)S(1)}, u32[]{:S(2)}, u32[]{:S(2)}) collective-permute-start(f32[2,32,1,128]{3,2,1,0:T(1,128)S(1)} %get-tuple-element.127), channel_id=1, source_target_pairs={{0,4},{4,8},{8,12},{12,0},{1,5},{5,9},{9,13},{13,1},{2,6},{6,10},{... | collective-permute-start | bytes 98312 | tf_op jit(solution)/shard_map/ppermute | solution.py:24
  13.2 176.9 %collective-permute-start.5 = (f32[2,32,32,1]{2,1,3,0:T(8,128)S(1)}, f32[2,32,32,1]{2,1,3,0:T(8,128)S(1)}, u32[]{:S(2)}, u32[]{:S(2)}) collective-permute-start(f32[2,32,32,1]{2,1,3,0:T(8,128)S(1)} %copy.54), channel_id=1, source_target_pairs={{0,1},{1,2},{2,3},{3,0},{4,5},{5,6},{6,7},{7,4},{8,9},{9,10},{10,1... | collective-permute-start | bytes 24584 | tf_op jit(solution)/shard_map/ppermute | solution.py:24
  15.5 171.5 %collective-permute-start.4 = (f32[2,32,32,1]{2,1,3,0:T(8,128)S(1)}, f32[2,32,32,1]{2,1,3,0:T(8,128)S(1)}, u32[]{:S(2)}, u32[]{:S(2)}) collective-permute-start(f32[2,32,32,1]{2,1,3,0:T(8,128)S(1)} %copy.53), channel_id=1, source_target_pairs={{1,0},{2,1},{3,2},{0,3},{5,4},{6,5},{7,6},{4,7},{9,8},{10,9},{11,1... | collective-permute-start | bytes 24584 | tf_op jit(solution)/shard_map/ppermute | solution.py:25
  197.6 11.2 %collective-permute-start.10 = (f32[2,32,32,1]{2,1,3,0:T(8,128)S(1)}, f32[2,32,32,1]{2,1,3,0:T(8,128)S(1)}, u32[]{:S(2)}, u32[]{:S(2)}) collective-permute-start(f32[2,32,32,1]{2,1,3,0:T(8,128)S(1)} %copy.13), channel_id=1, source_target_pairs={{1,0},{2,1},{3,2},{0,3},{5,4},{6,5},{7,6},{4,7},{9,8},{10,9},{11,1... | collective-permute-start | bytes 24584 | tf_op jit(solution)/shard_map/ppermute | solution.py:25
  199.0 142.8 %collective-permute-start.7 = (f32[2,1,32,128]{3,2,1,0:T(8,128)S(1)}, f32[2,1,32,128]{3,2,1,0:T(8,128)S(1)}, u32[]{:S(2)}, u32[]{:S(2)}) collective-permute-start(f32[2,1,32,128]{3,2,1,0:T(8,128)S(1)} %get-tuple-element.121), channel_id=1, source_target_pairs={{0,16},{16,32},{32,48},{48,64},{64,80},{80,96},{96,112},{112,0},{1... | collective-permute-start | bytes 98312 | tf_op jit(solution)/shard_map/ppermute | solution.py:24
  200.8 141.0 %collective-permute-start.6 = (f32[2,1,32,128]{3,2,1,0:T(8,128)S(1)}, f32[2,1,32,128]{3,2,1,0:T(8,128)S(1)}, u32[]{:S(2)}, u32[]{:S(2)}) collective-permute-start(f32[2,1,32,128]{3,2,1,0:T(8,128)S(1)} %get-tuple-element.122), channel_id=1, source_target_pairs={{16,0},{32,16},{48,32},{64,48},{80,64},{96,80},{112,96},{0,112},{1... | collective-permute-start | bytes 98312 | tf_op jit(solution)/shard_map/ppermute | solution.py:25
  204.5 137.2 %collective-permute-start.9 = (f32[2,32,1,128]{3,2,1,0:T(1,128)S(1)}, f32[2,32,1,128]{3,2,1,0:T(1,128)S(1)}, u32[]{:S(2)}, u32[]{:S(2)}) collective-permute-start(f32[2,32,1,128]{3,2,1,0:T(1,128)S(1)} %get-tuple-element.123), channel_id=1, source_target_pairs={{0,4},{4,8},{8,12},{12,0},{1,5},{5,9},{9,13},{13,1},{2,6},{6,10},{... | collective-permute-start | bytes 98312 | tf_op jit(solution)/shard_map/ppermute | solution.py:24
  204.5 137.2 %collective-permute-start.8 = (f32[2,32,1,128]{3,2,1,0:T(1,128)S(1)}, f32[2,32,1,128]{3,2,1,0:T(1,128)S(1)}, u32[]{:S(2)}, u32[]{:S(2)}) collective-permute-start(f32[2,32,1,128]{3,2,1,0:T(1,128)S(1)} %get-tuple-element.124), channel_id=1, source_target_pairs={{4,0},{8,4},{12,8},{0,12},{5,1},{9,5},{13,9},{1,13},{6,2},{10,6},{... | collective-permute-start | bytes 98312 | tf_op jit(solution)/shard_map/ppermute | solution.py:25
  208.9 131.4 %collective-permute-start.11 = (f32[2,32,32,1]{2,1,3,0:T(8,128)S(1)}, f32[2,32,32,1]{2,1,3,0:T(8,128)S(1)}, u32[]{:S(2)}, u32[]{:S(2)}) collective-permute-start(f32[2,32,32,1]{2,1,3,0:T(8,128)S(1)} %copy.15), channel_id=1, source_target_pairs={{0,1},{1,2},{2,3},{3,0},{4,5},{5,6},{6,7},{7,4},{8,9},{9,10},{10,1... | collective-permute-start | bytes 24584 | tf_op jit(solution)/shard_map/ppermute | solution.py:24
  348.3 17.3 %collective-permute-start.13 = (f32[2,1,32,128]{3,2,1,0:T(8,128)S(1)}, f32[2,1,32,128]{3,2,1,0:T(8,128)S(1)}, u32[]{:S(2)}, u32[]{:S(2)}) collective-permute-start(f32[2,1,32,128]{3,2,1,0:T(8,128)S(1)} %get-tuple-element.115), channel_id=1, source_target_pairs={{0,16},{16,32},{32,48},{48,64},{64,80},{80,96},{96,112},{112,0},{1... | collective-permute-start | bytes 98312 | tf_op jit(solution)/shard_map/ppermute | solution.py:24
  348.5 17.1 %collective-permute-start.12 = (f32[2,1,32,128]{3,2,1,0:T(8,128)S(1)}, f32[2,1,32,128]{3,2,1,0:T(8,128)S(1)}, u32[]{:S(2)}, u32[]{:S(2)}) collective-permute-start(f32[2,1,32,128]{3,2,1,0:T(8,128)S(1)} %get-tuple-element.116), channel_id=1, source_target_pairs={{16,0},{32,16},{48,32},{64,48},{80,64},{96,80},{112,96},{0,112},{1... | collective-permute-start | bytes 98312 | tf_op jit(solution)/shard_map/ppermute | solution.py:25
  353.4 12.1 %collective-permute-start.15 = (f32[2,32,1,128]{3,2,1,0:T(1,128)S(1)}, f32[2,32,1,128]{3,2,1,0:T(1,128)S(1)}, u32[]{:S(2)}, u32[]{:S(2)}) collective-permute-start(f32[2,32,1,128]{3,2,1,0:T(1,128)S(1)} %get-tuple-element.117), channel_id=1, source_target_pairs={{0,4},{4,8},{8,12},{12,0},{1,5},{5,9},{9,13},{13,1},{2,6},{6,10},{... | collective-permute-start | bytes 98312 | tf_op jit(solution)/shard_map/ppermute | solution.py:24
  353.4 12.1 %collective-permute-start.14 = (f32[2,32,1,128]{3,2,1,0:T(1,128)S(1)}, f32[2,32,1,128]{3,2,1,0:T(1,128)S(1)}, u32[]{:S(2)}, u32[]{:S(2)}) collective-permute-start(f32[2,32,1,128]{3,2,1,0:T(1,128)S(1)} %get-tuple-element.118), channel_id=1, source_target_pairs={{4,0},{8,4},{12,8},{0,12},{5,1},{9,5},{13,9},{1,13},{6,2},{10,6},{... | collective-permute-start | bytes 98312 | tf_op jit(solution)/shard_map/ppermute | solution.py:25
  369.4 19.1 %collective-permute-start.19 = (f32[2,1,32,128]{3,2,1,0:T(8,128)S(1)}, f32[2,1,32,128]{3,2,1,0:T(8,128)S(1)}, u32[]{:S(2)}, u32[]{:S(2)}) collective-permute-start(f32[2,1,32,128]{3,2,1,0:T(8,128)S(1)} %get-tuple-element.111), channel_id=1, source_target_pairs={{0,16},{16,32},{32,48},{48,64},{64,80},{80,96},{96,112},{112,0},{1... | collective-permute-start | bytes 98312 | tf_op jit(solution)/shard_map/ppermute | solution.py:24
  369.5 19.0 %collective-permute-start.18 = (f32[2,1,32,128]{3,2,1,0:T(8,128)S(1)}, f32[2,1,32,128]{3,2,1,0:T(8,128)S(1)}, u32[]{:S(2)}, u32[]{:S(2)}) collective-permute-start(f32[2,1,32,128]{3,2,1,0:T(8,128)S(1)} %get-tuple-element.112), channel_id=1, source_target_pairs={{16,0},{32,16},{48,32},{64,48},{80,64},{96,80},{112,96},{0,112},{1... | collective-permute-start | bytes 98312 | tf_op jit(solution)/shard_map/ppermute | solution.py:25
  374.5 13.8 %collective-permute-start.21 = (f32[2,32,1,128]{3,2,1,0:T(1,128)S(1)}, f32[2,32,1,128]{3,2,1,0:T(1,128)S(1)}, u32[]{:S(2)}, u32[]{:S(2)}) collective-permute-start(f32[2,32,1,128]{3,2,1,0:T(1,128)S(1)} %get-tuple-element.109), channel_id=1, source_target_pairs={{0,4},{4,8},{8,12},{12,0},{1,5},{5,9},{9,13},{13,1},{2,6},{6,10},{... | collective-permute-start | bytes 98312 | tf_op jit(solution)/shard_map/ppermute | solution.py:24
  374.5 13.9 %collective-permute-start.20 = (f32[2,32,1,128]{3,2,1,0:T(1,128)S(1)}, f32[2,32,1,128]{3,2,1,0:T(1,128)S(1)}, u32[]{:S(2)}, u32[]{:S(2)}) collective-permute-start(f32[2,32,1,128]{3,2,1,0:T(1,128)S(1)} %get-tuple-element.110), channel_id=1, source_target_pairs={{4,0},{8,4},{12,8},{0,12},{5,1},{9,5},{13,9},{1,13},{6,2},{10,6},{... | collective-permute-start | bytes 98312 | tf_op jit(solution)/shard_map/ppermute | solution.py:25
  427.1 17.5 %collective-permute-start.25 = (f32[2,1,32,128]{3,2,1,0:T(8,128)S(1)}, f32[2,1,32,128]{3,2,1,0:T(8,128)S(1)}, u32[]{:S(2)}, u32[]{:S(2)}) collective-permute-start(f32[2,1,32,128]{3,2,1,0:T(8,128)S(1)} %get-tuple-element.103), channel_id=1, source_target_pairs={{0,16},{16,32},{32,48},{48,64},{64,80},{80,96},{96,112},{112,0},{1... | collective-permute-start | bytes 98312 | tf_op jit(solution)/shard_map/ppermute | solution.py:24
  427.5 17.1 %collective-permute-start.24 = (f32[2,1,32,128]{3,2,1,0:T(8,128)S(1)}, f32[2,1,32,128]{3,2,1,0:T(8,128)S(1)}, u32[]{:S(2)}, u32[]{:S(2)}) collective-permute-start(f32[2,1,32,128]{3,2,1,0:T(8,128)S(1)} %get-tuple-element.104), channel_id=1, source_target_pairs={{16,0},{32,16},{48,32},{64,48},{80,64},{96,80},{112,96},{0,112},{1... | collective-permute-start | bytes 98312 | tf_op jit(solution)/shard_map/ppermute | solution.py:25
  432.3 12.3 %collective-permute-start.27 = (f32[2,32,1,128]{3,2,1,0:T(1,128)S(1)}, f32[2,32,1,128]{3,2,1,0:T(1,128)S(1)}, u32[]{:S(2)}, u32[]{:S(2)}) collective-permute-start(f32[2,32,1,128]{3,2,1,0:T(1,128)S(1)} %get-tuple-element.105), channel_id=1, source_target_pairs={{0,4},{4,8},{8,12},{12,0},{1,5},{5,9},{9,13},{13,1},{2,6},{6,10},{... | collective-permute-start | bytes 98312 | tf_op jit(solution)/shard_map/ppermute | solution.py:24
  434.0 10.6 %collective-permute-start.26 = (f32[2,32,1,128]{3,2,1,0:T(1,128)S(1)}, f32[2,32,1,128]{3,2,1,0:T(1,128)S(1)}, u32[]{:S(2)}, u32[]{:S(2)}) collective-permute-start(f32[2,32,1,128]{3,2,1,0:T(1,128)S(1)} %get-tuple-element.106), channel_id=1, source_target_pairs={{4,0},{8,4},{12,8},{0,12},{5,1},{9,5},{13,9},{1,13},{6,2},{10,6},{... | collective-permute-start | bytes 98312 | tf_op jit(solution)/shard_map/ppermute | solution.py:25
  448.2 19.3 %collective-permute-start.31 = (f32[2,1,32,128]{3,2,1,0:T(8,128)S(1)}, f32[2,1,32,128]{3,2,1,0:T(8,128)S(1)}, u32[]{:S(2)}, u32[]{:S(2)}) collective-permute-start(f32[2,1,32,128]{3,2,1,0:T(8,128)S(1)} %get-tuple-element.99), channel_id=1, source_target_pairs={{0,16},{16,32},{32,48},{48,64},{64,80},{80,96},{96,112},{112,0},{1... | collective-permute-start | bytes 98312 | tf_op jit(solution)/shard_map/ppermute | solution.py:24
  448.3 19.3 %collective-permute-start.30 = (f32[2,1,32,128]{3,2,1,0:T(8,128)S(1)}, f32[2,1,32,128]{3,2,1,0:T(8,128)S(1)}, u32[]{:S(2)}, u32[]{:S(2)}) collective-permute-start(f32[2,1,32,128]{3,2,1,0:T(8,128)S(1)} %get-tuple-element.100), channel_id=1, source_target_pairs={{16,0},{32,16},{48,32},{64,48},{80,64},{96,80},{112,96},{0,112},{1... | collective-permute-start | bytes 98312 | tf_op jit(solution)/shard_map/ppermute | solution.py:25
  453.3 14.1 %collective-permute-start.33 = (f32[2,32,1,128]{3,2,1,0:T(1,128)S(1)}, f32[2,32,1,128]{3,2,1,0:T(1,128)S(1)}, u32[]{:S(2)}, u32[]{:S(2)}) collective-permute-start(f32[2,32,1,128]{3,2,1,0:T(1,128)S(1)} %get-tuple-element.97), channel_id=1, source_target_pairs={{0,4},{4,8},{8,12},{12,0},{1,5},{5,9},{9,13},{13,1},{2,6},{6,10},{... | collective-permute-start | bytes 98312 | tf_op jit(solution)/shard_map/ppermute | solution.py:24
  453.9 13.6 %collective-permute-start.32 = (f32[2,32,1,128]{3,2,1,0:T(1,128)S(1)}, f32[2,32,1,128]{3,2,1,0:T(1,128)S(1)}, u32[]{:S(2)}, u32[]{:S(2)}) collective-permute-start(f32[2,32,1,128]{3,2,1,0:T(1,128)S(1)} %get-tuple-element.98), channel_id=1, source_target_pairs={{4,0},{8,4},{12,8},{0,12},{5,1},{9,5},{13,9},{1,13},{6,2},{10,6},{... | collective-permute-start | bytes 98312 | tf_op jit(solution)/shard_map/ppermute | solution.py:25
  459.5 4.9 collective-permute-start.34
  506.6 18.5 %collective-permute-start.37 = (f32[2,1,32,128]{3,2,1,0:T(8,128)S(1)}, f32[2,1,32,128]{3,2,1,0:T(8,128)S(1)}, u32[]{:S(2)}, u32[]{:S(2)}) collective-permute-start(f32[2,1,32,128]{3,2,1,0:T(8,128)S(1)} %get-tuple-element.91), channel_id=1, source_target_pairs={{0,16},{16,32},{32,48},{48,64},{64,80},{80,96},{96,112},{112,0},{1... | collective-permute-start | bytes 98312 | tf_op jit(solution)/shard_map/ppermute | solution.py:24
  507.0 18.1 %collective-permute-start.36 = (f32[2,1,32,128]{3,2,1,0:T(8,128)S(1)}, f32[2,1,32,128]{3,2,1,0:T(8,128)S(1)}, u32[]{:S(2)}, u32[]{:S(2)}) collective-permute-start(f32[2,1,32,128]{3,2,1,0:T(8,128)S(1)} %get-tuple-element.92), channel_id=1, source_target_pairs={{16,0},{32,16},{48,32},{64,48},{80,64},{96,80},{112,96},{0,112},{1... | collective-permute-start | bytes 98312 | tf_op jit(solution)/shard_map/ppermute | solution.py:25
  511.8 13.3 %collective-permute-start.39 = (f32[2,32,1,128]{3,2,1,0:T(1,128)S(1)}, f32[2,32,1,128]{3,2,1,0:T(1,128)S(1)}, u32[]{:S(2)}, u32[]{:S(2)}) collective-permute-start(f32[2,32,1,128]{3,2,1,0:T(1,128)S(1)} %get-tuple-element.93), channel_id=1, source_target_pairs={{0,4},{4,8},{8,12},{12,0},{1,5},{5,9},{9,13},{13,1},{2,6},{6,10},{... | collective-permute-start | bytes 98312 | tf_op jit(solution)/shard_map/ppermute | solution.py:24
  513.5 11.6 %collective-permute-start.38 = (f32[2,32,1,128]{3,2,1,0:T(1,128)S(1)}, f32[2,32,1,128]{3,2,1,0:T(1,128)S(1)}, u32[]{:S(2)}, u32[]{:S(2)}) collective-permute-start(f32[2,32,1,128]{3,2,1,0:T(1,128)S(1)} %get-tuple-element.94), channel_id=1, source_target_pairs={{4,0},{8,4},{12,8},{0,12},{5,1},{9,5},{13,9},{1,13},{6,2},{10,6},{... | collective-permute-start | bytes 98312 | tf_op jit(solution)/shard_map/ppermute | solution.py:25
  528.9 19.0 %collective-permute-start.43 = (f32[2,1,32,128]{3,2,1,0:T(8,128)S(1)}, f32[2,1,32,128]{3,2,1,0:T(8,128)S(1)}, u32[]{:S(2)}, u32[]{:S(2)}) collective-permute-start(f32[2,1,32,128]{3,2,1,0:T(8,128)S(1)} %get-tuple-element.87), channel_id=1, source_target_pairs={{0,16},{16,32},{32,48},{48,64},{64,80},{80,96},{96,112},{112,0},{1... | collective-permute-start | bytes 98312 | tf_op jit(solution)/shard_map/ppermute | solution.py:24
  529.0 18.9 %collective-permute-start.42 = (f32[2,1,32,128]{3,2,1,0:T(8,128)S(1)}, f32[2,1,32,128]{3,2,1,0:T(8,128)S(1)}, u32[]{:S(2)}, u32[]{:S(2)}) collective-permute-start(f32[2,1,32,128]{3,2,1,0:T(8,128)S(1)} %get-tuple-element.88), channel_id=1, source_target_pairs={{16,0},{32,16},{48,32},{64,48},{80,64},{96,80},{112,96},{0,112},{1... | collective-permute-start | bytes 98312 | tf_op jit(solution)/shard_map/ppermute | solution.py:25
  534.0 13.7 %collective-permute-start.45 = (f32[2,32,1,128]{3,2,1,0:T(1,128)S(1)}, f32[2,32,1,128]{3,2,1,0:T(1,128)S(1)}, u32[]{:S(2)}, u32[]{:S(2)}) collective-permute-start(f32[2,32,1,128]{3,2,1,0:T(1,128)S(1)} %get-tuple-element.85), channel_id=1, source_target_pairs={{0,4},{4,8},{8,12},{12,0},{1,5},{5,9},{9,13},{13,1},{2,6},{6,10},{... | collective-permute-start | bytes 98312 | tf_op jit(solution)/shard_map/ppermute | solution.py:24
  534.6 13.3 %collective-permute-start.44 = (f32[2,32,1,128]{3,2,1,0:T(1,128)S(1)}, f32[2,32,1,128]{3,2,1,0:T(1,128)S(1)}, u32[]{:S(2)}, u32[]{:S(2)}) collective-permute-start(f32[2,32,1,128]{3,2,1,0:T(1,128)S(1)} %get-tuple-element.86), channel_id=1, source_target_pairs={{4,0},{8,4},{12,8},{0,12},{5,1},{9,5},{13,9},{1,13},{6,2},{10,6},{... | collective-permute-start | bytes 98312 | tf_op jit(solution)/shard_map/ppermute | solution.py:25
  587.8 18.2 %collective-permute-start.49 = (f32[2,1,32,128]{3,2,1,0:T(8,128)S(1)}, f32[2,1,32,128]{3,2,1,0:T(8,128)S(1)}, u32[]{:S(2)}, u32[]{:S(2)}) collective-permute-start(f32[2,1,32,128]{3,2,1,0:T(8,128)S(1)} %get-tuple-element.79), channel_id=1, source_target_pairs={{0,16},{16,32},{32,48},{48,64},{64,80},{80,96},{96,112},{112,0},{1... | collective-permute-start | bytes 98312 | tf_op jit(solution)/shard_map/ppermute | solution.py:24
  588.1 17.8 %collective-permute-start.48 = (f32[2,1,32,128]{3,2,1,0:T(8,128)S(1)}, f32[2,1,32,128]{3,2,1,0:T(8,128)S(1)}, u32[]{:S(2)}, u32[]{:S(2)}) collective-permute-start(f32[2,1,32,128]{3,2,1,0:T(8,128)S(1)} %get-tuple-element.80), channel_id=1, source_target_pairs={{16,0},{32,16},{48,32},{64,48},{80,64},{96,80},{112,96},{0,112},{1... | collective-permute-start | bytes 98312 | tf_op jit(solution)/shard_map/ppermute | solution.py:25
  592.9 13.0 %collective-permute-start.51 = (f32[2,32,1,128]{3,2,1,0:T(1,128)S(1)}, f32[2,32,1,128]{3,2,1,0:T(1,128)S(1)}, u32[]{:S(2)}, u32[]{:S(2)}) collective-permute-start(f32[2,32,1,128]{3,2,1,0:T(1,128)S(1)} %get-tuple-element.81), channel_id=1, source_target_pairs={{0,4},{4,8},{8,12},{12,0},{1,5},{5,9},{9,13},{13,1},{2,6},{6,10},{... | collective-permute-start | bytes 98312 | tf_op jit(solution)/shard_map/ppermute | solution.py:24
  594.7 11.3 %collective-permute-start.50 = (f32[2,32,1,128]{3,2,1,0:T(1,128)S(1)}, f32[2,32,1,128]{3,2,1,0:T(1,128)S(1)}, u32[]{:S(2)}, u32[]{:S(2)}) collective-permute-start(f32[2,32,1,128]{3,2,1,0:T(1,128)S(1)} %get-tuple-element.82), channel_id=1, source_target_pairs={{4,0},{8,4},{12,8},{0,12},{5,1},{9,5},{13,9},{1,13},{6,2},{10,6},{... | collective-permute-start | bytes 98312 | tf_op jit(solution)/shard_map/ppermute | solution.py:25
  612.0 19.0 %collective-permute-start.55 = (f32[2,1,32,128]{3,2,1,0:T(8,128)S(1)}, f32[2,1,32,128]{3,2,1,0:T(8,128)S(1)}, u32[]{:S(2)}, u32[]{:S(2)}) collective-permute-start(f32[2,1,32,128]{3,2,1,0:T(8,128)S(1)} %get-tuple-element.73), channel_id=1, source_target_pairs={{0,16},{16,32},{32,48},{48,64},{64,80},{80,96},{96,112},{112,0},{1... | collective-permute-start | bytes 98312 | tf_op jit(solution)/shard_map/ppermute | solution.py:24
  612.0 18.9 %collective-permute-start.54 = (f32[2,1,32,128]{3,2,1,0:T(8,128)S(1)}, f32[2,1,32,128]{3,2,1,0:T(8,128)S(1)}, u32[]{:S(2)}, u32[]{:S(2)}) collective-permute-start(f32[2,1,32,128]{3,2,1,0:T(8,128)S(1)} %get-tuple-element.74), channel_id=1, source_target_pairs={{16,0},{32,16},{48,32},{64,48},{80,64},{96,80},{112,96},{0,112},{1... | collective-permute-start | bytes 98312 | tf_op jit(solution)/shard_map/ppermute | solution.py:25
  617.1 13.7 %collective-permute-start.57 = (f32[2,32,1,128]{3,2,1,0:T(1,128)S(1)}, f32[2,32,1,128]{3,2,1,0:T(1,128)S(1)}, u32[]{:S(2)}, u32[]{:S(2)}) collective-permute-start(f32[2,32,1,128]{3,2,1,0:T(1,128)S(1)} %get-tuple-element.75), channel_id=1, source_target_pairs={{0,4},{4,8},{8,12},{12,0},{1,5},{5,9},{9,13},{13,1},{2,6},{6,10},{... | collective-permute-start | bytes 98312 | tf_op jit(solution)/shard_map/ppermute | solution.py:24
  617.6 13.2 %collective-permute-start.56 = (f32[2,32,1,128]{3,2,1,0:T(1,128)S(1)}, f32[2,32,1,128]{3,2,1,0:T(1,128)S(1)}, u32[]{:S(2)}, u32[]{:S(2)}) collective-permute-start(f32[2,32,1,128]{3,2,1,0:T(1,128)S(1)} %get-tuple-element.76), channel_id=1, source_target_pairs={{4,0},{8,4},{12,8},{0,12},{5,1},{9,5},{13,9},{1,13},{6,2},{10,6},{... | collective-permute-start | bytes 98312 | tf_op jit(solution)/shard_map/ppermute | solution.py:25
  670.1 22.3 %collective-permute-start.63 = (f32[4,32,1,128]{3,2,1,0:T(1,128)S(1)}, f32[4,32,1,128]{3,2,1,0:T(1,128)S(1)}, u32[]{:S(2)}, u32[]{:S(2)}) collective-permute-start(f32[4,32,1,128]{3,2,1,0:T(1,128)S(1)} %get-tuple-element.69), channel_id=1, source_target_pairs={{0,4},{4,8},{8,12},{12,0},{1,5},{5,9},{9,13},{13,1},{2,6},{6,10},{... | collective-permute-start | bytes 196616 | tf_op jit(solution)/shard_map/ppermute | solution.py:24
  671.9 20.5 %collective-permute-start.62 = (f32[4,32,1,128]{3,2,1,0:T(1,128)S(1)}, f32[4,32,1,128]{3,2,1,0:T(1,128)S(1)}, u32[]{:S(2)}, u32[]{:S(2)}) collective-permute-start(f32[4,32,1,128]{3,2,1,0:T(1,128)S(1)} %get-tuple-element.70), channel_id=1, source_target_pairs={{4,0},{8,4},{12,8},{0,12},{5,1},{9,5},{13,9},{1,13},{6,2},{10,6},{... | collective-permute-start | bytes 196616 | tf_op jit(solution)/shard_map/ppermute | solution.py:25
  672.8 19.6 %collective-permute-start.61 = (f32[4,1,32,128]{3,2,1,0:T(8,128)S(1)}, f32[4,1,32,128]{3,2,1,0:T(8,128)S(1)}, u32[]{:S(2)}, u32[]{:S(2)}) collective-permute-start(f32[4,1,32,128]{3,2,1,0:T(8,128)S(1)} %get-tuple-element.67), channel_id=1, source_target_pairs={{0,16},{16,32},{32,48},{48,64},{64,80},{80,96},{96,112},{112,0},{1... | collective-permute-start | bytes 196616 | tf_op jit(solution)/shard_map/ppermute | solution.py:24
  673.1 19.4 %collective-permute-start.60 = (f32[4,1,32,128]{3,2,1,0:T(8,128)S(1)}, f32[4,1,32,128]{3,2,1,0:T(8,128)S(1)}, u32[]{:S(2)}, u32[]{:S(2)}) collective-permute-start(f32[4,1,32,128]{3,2,1,0:T(8,128)S(1)} %get-tuple-element.68), channel_id=1, source_target_pairs={{16,0},{32,16},{48,32},{64,48},{80,64},{96,80},{112,96},{0,112},{1... | collective-permute-start | bytes 196616 | tf_op jit(solution)/shard_map/ppermute | solution.py:25
  (40 other events, 261.0 us)
where the time goes:
time: 707 us; the launch traced here: 701 us
  local copies, waits for them, and re-layouts  229 us (32%)
  other arithmetic  228 us (32%)
  blocking collectives  120 us (17%)
  starting transfers between devices  112 us (16%)
  waiting for transfers between devices  8.92 us (1%)
    unnamed x6, other arithmetic  156 us
    slice x1, local copies, waits for them, and re-layouts, on_device(): counted = scattered[0].reshape(field_shape)  128 us
    psum x20, blocking collectives, one_axis_at_a_time(): shard = lax.psum(shard, axis)  120 us
    ppermute x33, starting transfers between devices, padded_2(): lax.ppermute(leading, axis, [(b, a) for a, b in up])  92.8 us
    slice x21, local copies, waits for them, and re-layouts, padded_2(): leading = lax.slice_in_dim(shard, 0, width, axis=dim)  34.8 us
    reduce_sum x4, other arithmetic, two_products(): jnp.sum(residual * image, axis=(1, 2, 3))  27.4 us
    sub x6, other arithmetic, stencil(): return (kappa_sq[None] + 6.0) * center - beside  24.4 us
    ppermute x33, starting transfers between devices, padded_2(): lax.ppermute(last, axis, up)  19.4 us
  transfers between devices with their start and end apart: 66, of which 10 were waited for; matrix products, arithmetic and copies ran while one was open for 55% of the time, Pallas kernels for 0%

commit v1 on v0

v1 whole, which is shorter than its diff:
```python
import functools

import jax
import jax.numpy as jnp
from jax import lax
from jax.experimental import pallas as pl
from jax.experimental.pallas import tpu as pltpu
from jax.sharding import PartitionSpec as P

ITERS = 4
SETS = 2
LANES = 128
TOP = 8
MESH = pl.DeviceIdType.MESH
INV_NOISE = 4.0


def kernel(
    sizes,
    lr_hbm, st_hbm, x0_hbm, index_ref, value_ref,
    grad_ref, adj_ref,
    kap, fp, ft, fs, xx, ax, pp, ap, ss, qq, ww, bb, ast,
    ysp, yst, yss, zsp, zst, zss, yrp, yrt, yrs, zrp, zrt, zrs,
    onehot_lo, onehot_hi, ar1, ar2, mine1, mine2,
    send_sem, recv_sem, ar_send, ar_recv1, ar_recv2, local_sem,
):
    gx_n, gy_n, gz_n = sizes
    nx, ny = kap.shape[0], kap.shape[1]
    yb_n = ny // 8
    gx, gy, gz = lax.axis_index("gx"), lax.axis_index("gy"), lax.axis_index("gz")

    def around(dx, dy, dz):
        return (
            lax.rem(gx + dx + gx_n, gx_n),
            lax.rem(gy + dy + gy_n, gy_n),
            lax.rem(gz + dz + gz_n, gz_n),
        )

    plane = [(0, dy, dz) for dy in range(gy_n) for dz in range(gz_n) if (dy, dz) != (0, 0)]
    column = [(dx, 0, 0) for dx in range(1, gx_n)]

    inner = (slice(None), pl.ds(1, nx), pl.ds(TOP, ny), slice(None))
    loads = [
        pltpu.make_async_copy(x0_hbm, fp.at[inner], local_sem.at[0]),
        pltpu.make_async_copy(st_hbm, fs.at[inner], local_sem.at[1]),
        pltpu.make_async_copy(lr_hbm, kap, local_sem.at[2]),
        pltpu.make_async_copy(x0_hbm, xx, local_sem.at[3]),
    ]
    for load in loads:
        load.start()

    barrier = pltpu.get_barrier_semaphore()
    for offset in plane + column:
        pl.semaphore_signal(barrier, inc=1, device_id=around(*offset), device_id_type=MESH)

    lane = lax.broadcasted_iota(jnp.int32, (8, LANES), 1)
    sub = lax.broadcasted_iota(jnp.int32, (8, LANES), 0)
    pair = lane // 2
    even = lane % 2 == 0
    zero = jnp.zeros((8, LANES), jnp.float32)

    def faces(kind, field, ys, zs, yr, zr):
        moves = [
            (field.at[:, nx, pl.ds(TOP, ny), :], field.at[:, 0, pl.ds(TOP, ny), :], (1, 0, 0)),
            (field.at[:, 1, pl.ds(TOP, ny), :], field.at[:, nx + 1, pl.ds(TOP, ny), :], (-1, 0, 0)),
            (ys.at[1], yr.at[0], (0, 1, 0)),
            (ys.at[0], yr.at[1], (0, -1, 0)),
            (zs, zr.at[0], (0, 0, 1)),
            (zs, zr.at[1], (0, 0, -1)),
        ]
        return [
            pltpu.make_async_remote_copy(
                src_ref=src, dst_ref=dst, send_sem=send_sem.at[kind, k], recv_sem=recv_sem.at[kind, k],
                device_id=around(*offset), device_id_type=MESH,
            )
            for k, (src, dst, offset) in enumerate(moves)
        ]

    def start(copies):
        for k in (4, 5, 2, 3, 0, 1):
            copies[k].start()

    def keep_rows(ys, s, x, yb, tile):
        if yb == 0:
            ys[0, s, pl.ds(x, 1), :] = tile[0:1, :]
        if yb == yb_n - 1:
            ys[1, s, pl.ds(x, 1), :] = tile[7:8, :]

    def packed(acc, s, x, tile):
        j = s * nx + x
        return jnp.where(pair == j, pltpu.roll(tile, 2 * j + 1, 1), acc)

    def put_packed(zs, acc):
        for yb in range(yb_n):
            zs[8 * yb : 8 * yb + 8, :] = acc[yb]

    def sweep(body, carry, lo, hi, unroll=1):
        return lax.fori_loop(lo, hi, body, carry, unroll=unroll)

    def face_pass(field, ys, zs):
        def body(x, acc):
            acc = list(acc)
            for s in range(SETS):
                for yb in range(yb_n):
                    tile = field[s, x + 1, TOP + 8 * yb : TOP + 8 * yb + 8, :]
                    keep_rows(ys, s, x, yb, tile)
                    acc[yb] = packed(acc[yb], s, x, tile)
            return tuple(acc)
        put_packed(zs, sweep(body, (zero,) * yb_n, 0, nx))

    def apply(field, copies, yr, zr, emit, carry, between=None):
        for k in (2, 3, 4, 5):
            copies[k].wait_recv()
        zc = [
            jnp.where(even, zr[0, 8 * yb : 8 * yb + 8, :], zr[1, 8 * yb : 8 * yb + 8, :])
            for yb in range(yb_n)
        ]

        def body(x, carry):
            for s in range(SETS):
                j = s * nx + x
                for yb in range(yb_n):
                    r = TOP + 8 * yb
                    c = field[s, x + 1, r : r + 8, :]
                    xs = field[s, x, r : r + 8, :] + field[s, x + 2, r : r + 8, :]
                    ym = field[s, x + 1, r - 1 : r + 7, :]
                    yp = field[s, x + 1, r + 1 : r + 9, :]
                    if yb == 0:
                        ym = jnp.where(sub == 0, yr[0, s, pl.ds(x, 1), :], ym)
                    if yb == yb_n - 1:
                        yp = jnp.where(sub == 7, yr[1, s, pl.ds(x, 1), :], yp)
                    h = pltpu.roll(zc[yb], LANES - 1 - 2 * j, 1)
                    zm = pltpu.roll(jnp.where(lane == LANES - 1, h, c), 1, 1)
                    zp = pltpu.roll(jnp.where(lane == 0, h, c), LANES - 1, 1)
                    beside = xs + (ym + yp) + (zm + zp)
                    out = (kap[x, 8 * yb : 8 * yb + 8, :] + 6.0) * c - beside
                    carry = emit(s, x, yb, c, out, carry)
            return carry

        carry = sweep(body, carry, 1, nx - 1)
        if between is not None:
            between()
        for k in (0, 1):
            copies[k].wait_recv()
        carry = body(0, carry)
        carry = body(nx - 1, carry)
        for copy in copies:
            copy.wait_send()
        return carry

    p_kind = (fp, ysp, zsp, yrp, zrp)
    t_kind = (ft, yst, zst, yrt, zrt)
    s_kind = (fs, yss, zss, yrs, zrs)

    loads[0].wait()
    face_pass(fp, ysp, zsp)
    pl.semaphore_wait(barrier, len(plane) + len(column))
    p_copies = faces(0, *p_kind)
    start(p_copies)
    loads[1].wait()
    face_pass(fs, yss, zss)
    s_copies = faces(2, *s_kind)
    start(s_copies)
    loads[2].wait()
    loads[3].wait()

    def kappa(x, _):
        kap[x] = 4.0 * jnp.exp(-2.0 * kap[x])
        return _
    sweep(kappa, 0, 0, nx)

    nobs = index_ref.shape[1]
    rows = onehot_hi.shape[0]
    step = 512
    planes = rows // ny

    def observe(s):
        for k in range(0, nobs, step):
            low = index_ref[s : s + 1, k : k + step] % LANES
            v = value_ref[s : s + 1, k : k + step]
            v1 = v.astype(jnp.bfloat16).astype(jnp.float32)
            v2 = (v - v1).astype(jnp.bfloat16).astype(jnp.float32)
            v3 = v - v1 - v2
            hit = lax.broadcasted_iota(jnp.int32, (LANES, step), 0) == low
            for n, weight in enumerate((jnp.ones_like(v), v1, v2, v3)):
                onehot_lo[LANES * n : LANES * (n + 1), k : k + step] = jnp.where(
                    hit, weight, 0.0
                ).astype(jnp.bfloat16)

        def body(m, _):
            for k in range(0, nobs, step):
                high = index_ref[s : s + 1, k : k + step] // LANES - m * rows
                onehot_hi[:, k : k + step] = jnp.where(
                    lax.broadcasted_iota(jnp.int32, (rows, step), 0) == high, 1.0, 0.0
                ).astype(jnp.bfloat16)
            sums = lax.dot_general(
                onehot_hi[...], onehot_lo[...], (((1,), (1,)), ((), ())),
                preferred_element_type=jnp.float32,
            )
            count = sums[:, :LANES].reshape(planes, ny, LANES)
            total = (sums[:, LANES : 2 * LANES] + sums[:, 2 * LANES : 3 * LANES]) + sums[:, 3 * LANES :]
            total = total.reshape(planes, ny, LANES)
            x = m * planes
            ww[s, pl.ds(x, planes)] = INV_NOISE * count
            bb[s, pl.ds(x, planes)] = INV_NOISE * (
                total - count * fs[s, pl.ds(x + 1, planes), TOP : TOP + ny, :]
            )
            return _
        sweep(body, 0, 0, nx // planes)

    observe(0)

    def rows_of(yb):
        return slice(8 * yb, 8 * yb + 8)

    def inner_rows(yb):
        return slice(TOP + 8 * yb, TOP + 8 * yb + 8)

    def emit_start(s, x, yb, c, out, acc):
        ft[s, x + 1, inner_rows(yb), :] = out
        ax[s, x, rows_of(yb), :] = out
        keep_rows(yst, s, x, yb, out)
        acc = list(acc)
        acc[yb] = packed(acc[yb], s, x, out)
        return tuple(acc)

    acc = apply(fp, p_copies, yrp, zrp, emit_start, (zero,) * yb_n)
    put_packed(zst, acc)
    t_copies = faces(1, *t_kind)
    start(t_copies)

    observe(1)

    def emit_state(s, x, yb, c, out, carry):
        ast[s, x, rows_of(yb), :] = out
        return carry
    apply(fs, s_copies, yrs, zrs, emit_state, 0)

    def emit_residual(s, x, yb, c, out, acc):
        v = fp[s, x + 1, inner_rows(yb), :]
        r = bb[s, x, rows_of(yb), :] - (out + ww[s, x, rows_of(yb), :] * v)
        fp[s, x + 1, inner_rows(yb), :] = r
        keep_rows(ysp, s, x, yb, r)
        acc = list(acc)
        acc[yb] = packed(acc[yb], s, x, r)
        return tuple(acc)

    acc = apply(ft, t_copies, yrt, zrt, emit_residual, (zero,) * yb_n)
    put_packed(zsp, acc)
    p_copies = faces(0, *p_kind)
    start(p_copies)

    def emit_first(s, x, yb, c, out, carry):
        ft[s, x + 1, inner_rows(yb), :] = out
        keep_rows(yst, s, x, yb, out)
        acc, sums = list(carry[0]), list(carry[1])
        acc[yb] = packed(acc[yb], s, x, out)
        square = c * c
        sums[s] = sums[s] + square
        sums[SETS + s] = sums[SETS + s] + (out * out + ww[s, x, rows_of(yb), :] * square)
        return (tuple(acc), tuple(sums))

    def emit_second(s, x, yb, c, out, carry):
        qq[s, x, rows_of(yb), :] = out + ww[s, x, rows_of(yb), :] * fp[s, x + 1, inner_rows(yb), :]
        return carry

    me1 = gy * gz_n + gz
    me2 = gx
    lane_row = lax.broadcasted_iota(jnp.int32, (1, LANES), 1)

    def first_stage(i, sums):
        row = jnp.zeros((1, LANES), jnp.float32)
        for n, part in enumerate(sums):
            total = jnp.sum(jnp.sum(part, axis=0, keepdims=True), axis=1, keepdims=True)
            row = jnp.where(lane_row == n, total, row)
        mine1[i] = row
        ar1[i, me1] = row
        copies = [
            pltpu.make_async_remote_copy(
                src_ref=mine1.at[i], dst_ref=ar1.at[i, me1], send_sem=ar_send.at[k],
                recv_sem=ar_recv1.at[i, k], device_id=around(*offset), device_id_type=MESH,
            )
            for k, offset in enumerate(plane)
        ]
        for copy in copies:
            copy.start()
        return copies

    def second_stage(i, copies):
        for copy in copies:
            copy.wait_recv()
        row = jnp.sum(ar1[i], axis=0)
        mine2[i] = row
        ar2[i, me2] = row
        later = [
            pltpu.make_async_remote_copy(
                src_ref=mine2.at[i], dst_ref=ar2.at[i, me2], send_sem=ar_send.at[len(plane) + k],
                recv_sem=ar_recv2.at[i, k], device_id=around(*offset), device_id_type=MESH,
            )
            for k, offset in enumerate(column)
        ]
        for copy in later:
            copy.start()
        return later

    def last_stage(i, copies, later):
        for copy in later:
            copy.wait_recv()
        row = jnp.sum(ar2[i], axis=0)
        for copy in copies + later:
            copy.wait_send()
        return [
            jnp.sum(jnp.where(lane_row == n, row, 0.0), axis=1, keepdims=True) for n in range(2 * SETS)
        ]

    norm_was = step_was = None
    for i in range(ITERS):
        acc, sums = apply(
            fp, p_copies, yrp, zrp, emit_first, ((zero,) * yb_n, (zero,) * (2 * SETS))
        )
        put_packed(zst, acc)
        copies = first_stage(i, sums)
        if i + 1 < ITERS:
            t_copies = faces(1, *t_kind)
            start(t_copies)
            box = []
            apply(ft, t_copies, yrt, zrt, emit_second, 0, lambda: box.append(second_stage(i, copies)))
            later = box[0]
        else:
            later = second_stage(i, copies)
        totals = last_stage(i, copies, later)
        norm, product = totals[:SETS], totals[SETS:]
        if i == 0:
            ratio = [None] * SETS
            size = [n / d for n, d in zip(norm, product)]
        else:
            ratio = [n / w for n, w in zip(norm, norm_was)]
            size = [n / (d - b * n / a) for n, d, b, a in zip(norm, product, ratio, step_was)]
        norm_was, step_was = norm, size
        beta = [None if b is None else jnp.broadcast_to(b, (8, LANES)) for b in ratio]
        alpha = [jnp.broadcast_to(a, (8, LANES)) for a in size]

        if i + 1 < ITERS:
            def advance(x, acc):
                acc = list(acc)
                for s in range(SETS):
                    for yb in range(yb_n):
                        rows_ = rows_of(yb)
                        r = fp[s, x + 1, inner_rows(yb), :]
                        p, image = r, qq[s, x, rows_, :]
                        if i > 0:
                            p = r + beta[s] * pp[s, x, rows_, :]
                            image = image + beta[s] * ss[s, x, rows_, :]
                        pp[s, x, rows_, :] = p
                        ss[s, x, rows_, :] = image
                        r = r - alpha[s] * image
                        fp[s, x + 1, inner_rows(yb), :] = r
                        keep_rows(ysp, s, x, yb, r)
                        acc[yb] = packed(acc[yb], s, x, r)
                return tuple(acc)
            put_packed(zsp, sweep(advance, (zero,) * yb_n, 0, nx))
            p_copies = faces(0, *p_kind)
            start(p_copies)

            def settle(x, _):
                for s in range(SETS):
                    for yb in range(yb_n):
                        rows_ = rows_of(yb)
                        applied = ft[s, x + 1, inner_rows(yb), :]
                        if i > 0:
                            applied = applied + beta[s] * ap[s, x, rows_, :]
                        ap[s, x, rows_, :] = applied
                        ax[s, x, rows_, :] += alpha[s] * applied
                        xx[s, x, rows_, :] += alpha[s] * pp[s, x, rows_, :]
                return _
            sweep(settle, 0, 0, nx)
        else:
            def finish(x, _):
                for yb in range(yb_n):
                    rows_ = rows_of(yb)
                    total = zero
                    for s in range(SETS):
                        p = fp[s, x + 1, inner_rows(yb), :] + beta[s] * pp[s, x, rows_, :]
                        applied = ft[s, x + 1, inner_rows(yb), :] + beta[s] * ap[s, x, rows_, :]
                        adjoint = xx[s, x, rows_, :] + alpha[s] * p
                        applied = ax[s, x, rows_, :] + alpha[s] * applied
                        adj_ref[s, x, rows_, :] = adjoint
                        total = total + (
                            adjoint * ast[s, x, rows_, :] + applied * fs[s, x + 1, inner_rows(yb), :]
                        )
                    grad_ref[x, rows_, :] = -2.0 * kap[x, rows_, :] * total
                return _
            sweep(finish, 0, 0, nx)


def on_device(sizes, log_range, state, adjoint_start, obs_index, obs_value):
    nx, ny, nz = log_range.shape
    nobs = obs_index.shape[-1]
    f32 = jnp.float32
    field = pltpu.VMEM((SETS, nx, ny, nz), f32)
    padded = pltpu.VMEM((SETS, nx + 2, ny + 2 * TOP, nz), f32)
    yface = pltpu.VMEM((2, SETS, nx, nz), f32)
    zsent = pltpu.VMEM((ny, LANES), f32)
    zgot = pltpu.VMEM((2, ny, LANES), f32)
    group = sizes[1] * sizes[2]
    vmem = pl.BlockSpec(memory_space=pltpu.VMEM)
    hbm = pl.BlockSpec(memory_space=pl.ANY)
    dma = pltpu.SemaphoreType.DMA
    return pl.pallas_call(
        functools.partial(kernel, sizes),
        out_shape=(
            jax.ShapeDtypeStruct((nx, ny, nz), f32),
            jax.ShapeDtypeStruct((SETS, nx, ny, nz), f32),
        ),
        in_specs=[hbm, hbm, hbm, vmem, vmem],
        out_specs=(vmem, vmem),
        scratch_shapes=[
            pltpu.VMEM((nx, ny, nz), f32),
            padded, padded, padded,
            field, field, field, field, field, field, field, field, field,
            yface, yface, yface, zsent, zsent, zsent, yface, yface, yface, zgot, zgot, zgot,
            pltpu.VMEM((4 * LANES, nobs), jnp.bfloat16),
            pltpu.VMEM((256, nobs), jnp.bfloat16),
            pltpu.VMEM((ITERS, group, 1, LANES), f32),
            pltpu.VMEM((ITERS, sizes[0], 1, LANES), f32),
            pltpu.VMEM((ITERS, 1, LANES), f32),
            pltpu.VMEM((ITERS, 1, LANES), f32),
            dma((3, 6)), dma((3, 6)),
            dma((group + sizes[0] - 2,)),
            dma((ITERS, group - 1)), dma((ITERS, sizes[0] - 1)),
            dma((4,)),
        ],
        compiler_params=pltpu.CompilerParams(
            collective_id=0, has_side_effects=True, vmem_limit_bytes=60 * 1024 * 1024
        ),
    )(
        log_range, state, adjoint_start,
        obs_index.reshape(SETS, nobs), obs_value.reshape(SETS, nobs),
    )


def solution(mesh):
    sizes = (mesh.shape["gx"], mesh.shape["gy"], mesh.shape["gz"])
    whole, per_set = P("gx", "gy", "gz"), P(None, "gx", "gy", "gz")
    obs = P(None, "gx", "gy", "gz", None)
    return jax.shard_map(
        functools.partial(on_device, sizes), mesh=mesh,
        in_specs=(whole, per_set, per_set, obs, obs), out_specs=(whole, per_set), check_vma=False,
    )
```

time: 707 us -> 149 us (0.21)
  other arithmetic: 228 us -> 0 us
  local copies, waits for them, and re-layouts: 229 us -> 4.98 us
  Pallas kernels: 0 us -> 143 us
  blocking collectives: 120 us -> 0 us
  starting transfers between devices: 112 us -> 0 us
  waiting for transfers between devices: 8.92 us -> 0 us
    slice x51 -> x0, local copies, waits for them, and re-layouts: 180 us -> none  [the longest x1 128 us: on_device(): counted = scattered[0].reshape(field_shape)]
    unnamed x6 -> x0, other arithmetic: 156 us -> none
    pallas_call x0 -> x1, Pallas kernels: none -> 143 us  [on_device(): pl.pallas_call(functools.partial(kernel, sizes), out_shape=(jax.ShapeDtyp...]
    psum x20 -> x0, blocking collectives: 120 us -> none  [one_axis_at_a_time(): shard = lax.psum(shard, axis)]
    ppermute x66 -> x0, starting transfers between devices: 112 us -> none  [the longest x33 92.8 us: padded_2(): lax.ppermute(leading, axis, [(b, a) for a, b in up])]
    sub x9 -> x0, other arithmetic: 34.2 us -> none  [the longest x6 24.4 us: stencil(): return (kappa_sq[None] + 6.0) * center - beside]
    ppermute x22 -> x0, local copies, waits for them, and re-layouts: 32.2 us -> none  [the longest x11 16.5 us: padded_2(): lax.ppermute(last, axis, up)]
    reduce_sum x6 -> x0, other arithmetic: 31.2 us -> none  [the longest x4 27.4 us: two_products(): jnp.sum(residual * image, axis=(1, 2, 3))]
  transfers between devices with their start and end apart: 66 -> 0, of which waited for: 10 -> 0; matrix products, arithmetic and copies ran while one was open for 55% -> 0% of each run, Pallas kernels for 0% -> 0%
where the time goes in v1:
time: 149 us
  Pallas kernels  143 us (96%)
  local copies, waits for them, and re-layouts  4.98 us (3%)
    pallas_call x1, Pallas kernels, on_device(): pl.pallas_call(functools.partial(kernel, sizes), out_shape=(jax.ShapeDtyp...  143 us
    unnamed x8, local copies, waits for them, and re-layouts  4.98 us

profile of v1, /device:TPU:1, one launch (start us, length us, event | category | flops | bytes accessed | tf_op | source)
XLA Modules:
  0.0 149.0 jit_solution(14175960694579225710)
XLA Ops:
  0.6 0.0 copy-start.1
  0.6 1.4 copy.12
  2.0 0.0 copy-done.1
  2.0 0.6 copy.11
  2.7 143.4 %shard_map.68 = (f32[32,32,128]{2,1,0:T(8,128)}, f32[2,32,32,128]{3,2,1,0:T(8,128)}) custom-call(f32[32,32,128]{2,1,0:T(8,128)} %lr_hbm.1, f32[2,32,32,128]{3,2,1,0:T(8,128)} %st_hbm.1, f32[2,32,32,128]{3,2,1,0:T(8,128)} %x0_hbm.1, s32[2,4096]{1,0:T(2,128)} %bitcast.6, f32[2,4096]{1,0:T(2,128)} %bitcast.7), custom_call_target="tpu_custom_call" | custom-call | tf_op jit(solution)/shard_map/pallas_call | solution.py:409
  146.1 0.0 copy-start
  146.1 2.0 %copy.15 = f32[32,32,128]{2,1,0:T(8,128)} copy(f32[32,32,128]{2,1,0:T(8,128)} %get-tuple-element.4) | data formatting | bytes 1048576
  148.1 0.0 copy-done
  148.1 1.0 copy.16
Async XLA Ops:
  0.6 1.4 copy-start.1
  146.1 2.0 %copy-start = (f32[2,32,32,128]{3,2,1,0:T(8,128)S(1)}, f32[2,32,32,128]{3,2,1,0:T(8,128)}, u32[]{:S(2)}) copy-start(f32[2,32,32,128]{3,2,1,0:T(8,128)} %get-tuple-element.5) | copy-start | bytes 3145732

commit v2 on v1

v2 whole, which is shorter than its diff:
```python
import functools

import jax
import jax.numpy as jnp
from jax import lax
from jax.experimental import pallas as pl
from jax.experimental.pallas import tpu as pltpu
from jax.sharding import PartitionSpec as P

ITERS = 4
SETS = 2
LANES = 128
TOP = 8
MESH = pl.DeviceIdType.MESH
INTERIOR = 6
WHOLE = 8
INV_NOISE = 4.0


def kernel(
    sizes,
    lr_hbm, st_hbm, x0_hbm, index_ref, value_ref,
    grad_ref, adj_ref,
    kap, fp, ft, fs, part, xx, ax, pp, ap, ss, sa, rr, ra, zz, ww, bb, ast,
    ysp, yst, yss, zsp, zst, zss, yrp, yrt, yrs, zrp, zrt, zrs,
    onehot_lo, onehot_hi, ar1, ar2, mine1, mine2,
    send_sem, recv_sem, ar_send, ar_recv1, ar_recv2, local_sem,
):
    gx_n, gy_n, gz_n = sizes
    nx, ny = kap.shape[0], kap.shape[1]
    yb_n = ny // 8
    gx, gy, gz = lax.axis_index("gx"), lax.axis_index("gy"), lax.axis_index("gz")

    def around(dx, dy, dz):
        return (
            lax.rem(gx + dx + gx_n, gx_n),
            lax.rem(gy + dy + gy_n, gy_n),
            lax.rem(gz + dz + gz_n, gz_n),
        )

    plane = [(0, dy, dz) for dy in range(gy_n) for dz in range(gz_n) if (dy, dz) != (0, 0)]
    column = [(dx, 0, 0) for dx in range(1, gx_n)]

    inner = (slice(None), pl.ds(1, nx), pl.ds(TOP, ny), slice(None))
    loads = [
        pltpu.make_async_copy(x0_hbm, fp.at[inner], local_sem.at[0]),
        pltpu.make_async_copy(st_hbm, fs.at[inner], local_sem.at[1]),
        pltpu.make_async_copy(lr_hbm, kap, local_sem.at[2]),
        pltpu.make_async_copy(x0_hbm, xx, local_sem.at[3]),
    ]
    for load in loads:
        load.start()

    barrier = pltpu.get_barrier_semaphore()
    for offset in plane + column:
        pl.semaphore_signal(barrier, inc=1, device_id=around(*offset), device_id_type=MESH)

    lane = lax.broadcasted_iota(jnp.int32, (8, LANES), 1)
    sub = lax.broadcasted_iota(jnp.int32, (8, LANES), 0)
    pair = lane // 2
    even = lane % 2 == 0
    zero = jnp.zeros((8, LANES), jnp.float32)

    def faces(kind, field, ys, zs, yr, zr):
        moves = [
            (field.at[:, nx, pl.ds(TOP, ny), :], field.at[:, 0, pl.ds(TOP, ny), :], (1, 0, 0)),
            (field.at[:, 1, pl.ds(TOP, ny), :], field.at[:, nx + 1, pl.ds(TOP, ny), :], (-1, 0, 0)),
            (ys.at[1], yr.at[0], (0, 1, 0)),
            (ys.at[0], yr.at[1], (0, -1, 0)),
            (zs, zr.at[0], (0, 0, 1)),
            (zs, zr.at[1], (0, 0, -1)),
        ]
        return [
            pltpu.make_async_remote_copy(
                src_ref=src, dst_ref=dst, send_sem=send_sem.at[kind, k], recv_sem=recv_sem.at[kind, k],
                device_id=around(*offset), device_id_type=MESH,
            )
            for k, (src, dst, offset) in enumerate(moves)
        ]

    def start(copies):
        for k in (4, 5, 2, 3, 0, 1):
            copies[k].start()

    def keep_rows(ys, s, x, yb, tile):
        if yb == 0:
            ys[0, s, pl.ds(x, 1), :] = tile[0:1, :]
        if yb == yb_n - 1:
            ys[1, s, pl.ds(x, 1), :] = tile[7:8, :]

    def packed(acc, s, x, tile):
        j = s * nx + x
        return jnp.where(pair == j, pltpu.roll(tile, 2 * j + 1, 1), acc)

    def put_packed(zs, acc):
        for yb in range(yb_n):
            zs[8 * yb : 8 * yb + 8, :] = acc[yb]

    def sweep(body, carry, lo, hi, unroll=1):
        def several(n, carry):
            for k in range(unroll):
                carry = body(lo + n * unroll + k, carry)
            return carry
        return lax.fori_loop(0, (hi - lo) // unroll, several, carry)

    def face_pass(field, ys, zs):
        def body(x, acc):
            acc = list(acc)
            for s in range(SETS):
                for yb in range(yb_n):
                    tile = field[s, x + 1, TOP + 8 * yb : TOP + 8 * yb + 8, :]
                    keep_rows(ys, s, x, yb, tile)
                    acc[yb] = packed(acc[yb], s, x, tile)
            return tuple(acc)
        put_packed(zs, sweep(body, (zero,) * yb_n, 0, nx, WHOLE))

    def rows_of(yb):
        return slice(8 * yb, 8 * yb + 8)

    def inner_rows(yb):
        return slice(TOP + 8 * yb, TOP + 8 * yb + 8)

    sides = (lane == 0) | (lane == LANES - 1)

    def apply(field, copies, yr, zr, emit, carry, gap=None, mid=None, part=part):
        def partial(x, _, lower=True, upper=True):
            for s in range(SETS):
                for yb in range(yb_n):
                    r = TOP + 8 * yb
                    c = field[s, x + 1, r : r + 8, :]
                    ym = field[s, x + 1, r - 1 : r + 7, :]
                    yp = field[s, x + 1, r + 1 : r + 9, :]
                    if yb == 0:
                        ym = jnp.where(sub == 0, 0.0, ym)
                    if yb == yb_n - 1:
                        yp = jnp.where(sub == 7, 0.0, yp)
                    zm = jnp.where(lane == 0, 0.0, pltpu.roll(c, 1, 1))
                    zp = jnp.where(lane == LANES - 1, 0.0, pltpu.roll(c, LANES - 1, 1))
                    beside = (ym + yp) + (zm + zp)
                    if lower:
                        beside = beside + field[s, x, r : r + 8, :]
                    if upper:
                        beside = beside + field[s, x + 2, r : r + 8, :]
                    part[s, x, rows_of(yb), :] = (kap[x, rows_of(yb), :] + 6.0) * c - beside
            return _

        partial(0, 0, lower=False)
        partial(nx - 1, 0, upper=False)
        sweep(partial, 0, 1, nx - 1, INTERIOR)
        if gap is not None:
            gap()
        for k in (2, 3, 4, 5):
            copies[k].wait_recv()
        zc = [
            jnp.where(even, zr[0, rows_of(yb), :], pltpu.roll(zr[1, rows_of(yb), :], LANES - 2, 1))
            for yb in range(yb_n)
        ]

        def complete(x, carry, slab=None):
            for s in range(SETS):
                shift = lax.rem(LANES - 2 * (s * nx + x), LANES)
                for yb in range(yb_n):
                    out = part[s, x, rows_of(yb), :]
                    out = out - jnp.where(sides, pltpu.roll(zc[yb], shift, 1), 0.0)
                    if yb == 0:
                        out = out - jnp.where(sub == 0, yr[0, s, pl.ds(x, 1), :], 0.0)
                    if yb == yb_n - 1:
                        out = out - jnp.where(sub == 7, yr[1, s, pl.ds(x, 1), :], 0.0)
                    if slab is not None:
                        out = out - field[s, slab, inner_rows(yb), :]
                    carry = emit(s, x, yb, out, carry)
            return carry

        carry = sweep(complete, carry, 1, nx - 1, INTERIOR)
        if mid is not None:
            mid()
        for k in (0, 1):
            copies[k].wait_recv()
        carry = complete(0, carry, 0)
        carry = complete(nx - 1, carry, nx + 1)
        for copy in copies:
            copy.wait_send()
        return carry

    p_kind = (fp, ysp, zsp, yrp, zrp)
    t_kind = (ft, yst, zst, yrt, zrt)
    s_kind = (fs, yss, zss, yrs, zrs)

    def kappa(x, _):
        kap[x] = 4.0 * jnp.exp(-2.0 * kap[x])
        return _

    nobs = index_ref.shape[2]
    rows = onehot_hi.shape[0]
    step = 512
    planes = rows // ny

    def build(s):
        for k in range(0, nobs, step):
            low = index_ref[s, :, k : k + step] % LANES
            v = value_ref[s, :, k : k + step]
            v1 = v.astype(jnp.bfloat16).astype(jnp.float32)
            v2 = (v - v1).astype(jnp.bfloat16).astype(jnp.float32)
            v3 = v - v1 - v2
            hit = lax.broadcasted_iota(jnp.int32, (LANES, step), 0) == low
            for n, weight in enumerate((jnp.ones_like(v), v1, v2, v3)):
                onehot_lo[LANES * n : LANES * (n + 1), k : k + step] = jnp.where(
                    hit, weight, 0.0
                ).astype(jnp.bfloat16)

    def observe(s, lo, hi):
        def body(m, _):
            for k in range(0, nobs, step):
                high = index_ref[s, :, k : k + step] // LANES - m * rows
                onehot_hi[:, k : k + step] = jnp.where(
                    lax.broadcasted_iota(jnp.int32, (rows, step), 0) == high, 1.0, 0.0
                ).astype(jnp.bfloat16)
            sums = lax.dot_general(
                onehot_hi[...], onehot_lo[...], (((1,), (1,)), ((), ())),
                preferred_element_type=jnp.float32,
            )
            count = sums[:, :LANES].reshape(planes, ny, LANES)
            total = (sums[:, LANES : 2 * LANES] + sums[:, 2 * LANES : 3 * LANES]) + sums[:, 3 * LANES :]
            total = total.reshape(planes, ny, LANES)
            x = m * planes
            ww[s, pl.ds(x, planes)] = INV_NOISE * count
            bb[s, pl.ds(x, planes)] = INV_NOISE * (
                total - count * fs[s, pl.ds(x + 1, planes), TOP : TOP + ny, :]
            )
            return _
        sweep(body, 0, lo, hi)

    me1 = gy * gz_n + gz
    me2 = gx
    lane_row = lax.broadcasted_iota(jnp.int32, (1, LANES), 1)

    def first_stage(i, sums):
        row = jnp.zeros((1, LANES), jnp.float32)
        for n, share in enumerate(sums):
            total = jnp.sum(jnp.sum(share, axis=0, keepdims=True), axis=1, keepdims=True)
            row = jnp.where(lane_row == n, total, row)
        mine1[i] = row
        ar1[i, me1] = row
        copies = [
            pltpu.make_async_remote_copy(
                src_ref=mine1.at[i], dst_ref=ar1.at[i, me1], send_sem=ar_send.at[k],
                recv_sem=ar_recv1.at[i, k], device_id=around(*offset), device_id_type=MESH,
            )
            for k, offset in enumerate(plane)
        ]
        for copy in copies:
            copy.start()
        return copies

    def second_stage(i, copies):
        for copy in copies:
            copy.wait_recv()
        row = jnp.sum(ar1[i], axis=0)
        mine2[i] = row
        ar2[i, me2] = row
        later = [
            pltpu.make_async_remote_copy(
                src_ref=mine2.at[i], dst_ref=ar2.at[i, me2], send_sem=ar_send.at[len(plane) + k],
                recv_sem=ar_recv2.at[i, k], device_id=around(*offset), device_id_type=MESH,
            )
            for k, offset in enumerate(column)
        ]
        for copy in later:
            copy.start()
        return copies + later

    def last_stage(i, copies):
        for copy in copies[len(plane) :]:
            copy.wait_recv()
        row = jnp.sum(ar2[i], axis=0)
        for copy in copies:
            copy.wait_send()
        return [
            jnp.sum(jnp.where(lane_row == n, row, 0.0), axis=1, keepdims=True) for n in range(2 * SETS)
        ]

    sums_of = {}
    norm, size, alpha, beta = {}, {}, {}, {}

    def middle(i):
        sums_of[i] = second_stage(i, sums_of[i])

    def scalars(i):
        totals = last_stage(i, sums_of[i])
        norm[i], product = totals[:SETS], totals[SETS:]
        if i == 0:
            size[i] = [n / d for n, d in zip(norm[i], product)]
        else:
            ratio = [n / w for n, w in zip(norm[i], norm[i - 1])]
            size[i] = [n / (d - b * n / a) for n, d, b, a in zip(norm[i], product, ratio, size[i - 1])]
            beta[i] = [jnp.broadcast_to(b, (8, LANES)) for b in ratio]
        alpha[i] = [jnp.broadcast_to(a, (8, LANES)) for a in size[i]]

    def advance(i):
        scalars(i)

        def body(x, sums):
            sums = list(sums)
            for s in range(SETS):
                for yb in range(yb_n):
                    at = (s, x, rows_of(yb), slice(None))
                    r, r_image = rr[at], ra[at]
                    p, p_image = r, r_image
                    q = fp[s, x + 1, inner_rows(yb), :]
                    q_image = ft[s, x + 1, inner_rows(yb), :]
                    if i > 0:
                        p = p + beta[i][s] * pp[at]
                        p_image = p_image + beta[i][s] * ap[at]
                        q = q + beta[i][s] * ss[at]
                        q_image = q_image + beta[i][s] * sa[at]
                    pp[at], ap[at] = p, p_image
                    if i + 2 < ITERS:
                        ss[at], sa[at] = q, q_image
                    xx[at] += alpha[i][s] * p
                    ax[at] += alpha[i][s] * p_image
                    r = r - alpha[i][s] * q
                    r_image = r_image - alpha[i][s] * q_image
                    rr[at], ra[at] = r, r_image
                    square = r * r
                    sums[s] = sums[s] + square
                    sums[SETS + s] = sums[SETS + s] + (r_image * r_image + ww[at] * square)
            return tuple(sums)
        sums_of[i + 1] = first_stage(i + 1, sweep(body, (zero,) * (2 * SETS), 0, nx, 2))

    no_faces = (zero,) * yb_n

    def sent(ys, s, x, yb, tile, acc):
        keep_rows(ys, s, x, yb, tile)
        acc = list(acc)
        acc[yb] = packed(acc[yb], s, x, tile)
        return tuple(acc)

    def send(kind, parts, acc):
        put_packed(parts[2], acc)
        copies = faces(kind, *parts)
        start(copies)
        return copies

    loads[0].wait()
    face_pass(fp, ysp, zsp)
    loads[2].wait()
    sweep(kappa, 0, 0, nx)
    loads[1].wait()
    face_pass(fs, yss, zss)
    loads[3].wait()
    build(0)
    observe(0, 0, 2)
    pl.semaphore_wait(barrier, len(plane) + len(column))
    p_copies = faces(0, *p_kind)
    start(p_copies)
    s_copies = faces(2, *s_kind)
    start(s_copies)

    def gap():
        observe(0, 2, 4)
        build(1)

    def emit_start(s, x, yb, out, acc):
        ft[s, x + 1, inner_rows(yb), :] = out
        ax[s, x, rows_of(yb), :] = out
        return sent(yst, s, x, yb, out, acc)

    t_copies = send(1, t_kind, apply(fp, p_copies, yrp, zrp, emit_start, no_faces, gap))

    def gap():
        observe(1, 0, 4)

    def emit_residual(s, x, yb, out, acc):
        at = (s, x, rows_of(yb), slice(None))
        r = bb[at] - (out + ww[at] * xx[at])
        rr[at] = r
        fp[s, x + 1, inner_rows(yb), :] = r
        return sent(ysp, s, x, yb, r, acc)

    p_copies = send(0, p_kind, apply(ft, t_copies, yrt, zrt, emit_residual, no_faces, gap))

    def emit_state(s, x, yb, out, carry):
        ast[s, x, rows_of(yb), :] = out
        return carry

    def emit_first(s, x, yb, out, carry):
        at = (s, x, rows_of(yb), slice(None))
        ft[s, x + 1, inner_rows(yb), :] = out
        ra[at] = out
        acc, sums = carry[0], list(carry[1])
        square = rr[at] * rr[at]
        sums[s] = sums[s] + square
        sums[SETS + s] = sums[SETS + s] + (out * out + ww[at] * square)
        return (sent(yst, s, x, yb, out, acc), tuple(sums))

    acc, sums = apply(fp, p_copies, yrp, zrp, emit_first, (no_faces, (zero,) * (2 * SETS)))
    sums_of[0] = first_stage(0, sums)
    t_copies = send(1, t_kind, acc)

    def emit_image(s, x, yb, out, acc):
        at = (s, x, rows_of(yb), slice(None))
        w = out + ww[at] * rr[at]
        fp[s, x + 1, inner_rows(yb), :] = w
        return sent(ysp, s, x, yb, w, acc)

    acc = apply(
        ft, t_copies, yrt, zrt, emit_image, no_faces,
        lambda: apply(fs, s_copies, yrs, zrs, emit_state, 0, part=ast), lambda: middle(0),
    )
    p_copies = send(0, p_kind, acc)

    for i in range(ITERS - 1):
        last = i + 2 == ITERS

        def emit_inner(s, x, yb, out, acc):
            ft[s, x + 1, inner_rows(yb), :] = out
            return acc if last else sent(yst, s, x, yb, out, acc)

        def emit_outer(s, x, yb, out, acc):
            at = (s, x, rows_of(yb), slice(None))
            w = fp[s, x + 1, inner_rows(yb), :]
            z = out + ww[at] * w
            if i > 0:
                z = z + beta[i][s] * zz[at]
            if i + 3 < ITERS:
                zz[at] = z
            w = w - alpha[i][s] * z
            fp[s, x + 1, inner_rows(yb), :] = w
            return sent(ysp, s, x, yb, w, acc)

        acc = apply(
            fp, p_copies, yrp, zrp, emit_inner, no_faces, None,
            None if i == 0 else functools.partial(middle, i),
        )
        if last:
            advance(i)
        else:
            t_copies = send(1, t_kind, acc)
            acc = apply(
                ft, t_copies, yrt, zrt, emit_outer, no_faces, functools.partial(advance, i)
            )
            p_copies = send(0, p_kind, acc)

    i = ITERS - 1
    middle(i)
    scalars(i)

    def finish(x, _):
        for yb in range(yb_n):
            total = zero
            for s in range(SETS):
                at = (s, x, rows_of(yb), slice(None))
                p = rr[at] + beta[i][s] * pp[at]
                p_image = ra[at] + beta[i][s] * ap[at]
                adjoint = xx[at] + alpha[i][s] * p
                image = ax[at] + alpha[i][s] * p_image
                adj_ref[at] = adjoint
                total = total + (adjoint * ast[at] + image * fs[s, x + 1, inner_rows(yb), :])
            grad_ref[x, rows_of(yb), :] = -2.0 * kap[x, rows_of(yb), :] * total
        return _
    sweep(finish, 0, 0, nx, 2)


def on_device(sizes, log_range, state, adjoint_start, obs_index, obs_value):
    nx, ny, nz = log_range.shape
    nobs = obs_index.shape[-1]
    f32 = jnp.float32
    field = pltpu.VMEM((SETS, nx, ny, nz), f32)
    padded = pltpu.VMEM((SETS, nx + 2, ny + 2 * TOP, nz), f32)
    yface = pltpu.VMEM((2, SETS, nx, nz), f32)
    zsent = pltpu.VMEM((ny, LANES), f32)
    zgot = pltpu.VMEM((2, ny, LANES), f32)
    group = sizes[1] * sizes[2]
    vmem = pl.BlockSpec(memory_space=pltpu.VMEM)
    hbm = pl.BlockSpec(memory_space=pl.ANY)
    dma = pltpu.SemaphoreType.DMA
    return pl.pallas_call(
        functools.partial(kernel, sizes),
        out_shape=(
            jax.ShapeDtypeStruct((nx, ny, nz), f32),
            jax.ShapeDtypeStruct((SETS, nx, ny, nz), f32),
        ),
        in_specs=[hbm, hbm, hbm, vmem, vmem],
        out_specs=(vmem, vmem),
        scratch_shapes=[
            pltpu.VMEM((nx, ny, nz), f32),
            padded, padded, padded,
            field, field, field, field, field, field, field, field, field, field, field, field, field,
            yface, yface, yface, zsent, zsent, zsent, yface, yface, yface, zgot, zgot, zgot,
            pltpu.VMEM((4 * LANES, nobs), jnp.bfloat16),
            pltpu.VMEM((256, nobs), jnp.bfloat16),
            pltpu.VMEM((ITERS, group, 1, LANES), f32),
            pltpu.VMEM((ITERS, sizes[0], 1, LANES), f32),
            pltpu.VMEM((ITERS, 1, LANES), f32),
            pltpu.VMEM((ITERS, 1, LANES), f32),
            dma((3, 6)), dma((3, 6)),
            dma((group + sizes[0] - 2,)),
            dma((ITERS, group - 1)), dma((ITERS, sizes[0] - 1)),
            dma((4,)),
        ],
        compiler_params=pltpu.CompilerParams(
            collective_id=0, has_side_effects=True, vmem_limit_bytes=60 * 1024 * 1024
        ),
    )(
        log_range, state, adjoint_start,
        obs_index.reshape(SETS, 1, nobs), obs_value.reshape(SETS, 1, nobs),
    )


def solution(mesh):
    sizes = (mesh.shape["gx"], mesh.shape["gy"], mesh.shape["gz"])
    whole, per_set = P("gx", "gy", "gz"), P(None, "gx", "gy", "gz")
    obs = P(None, "gx", "gy", "gz", None)
    return jax.shard_map(
        functools.partial(on_device, sizes), mesh=mesh,
        in_specs=(whole, per_set, per_set, obs, obs), out_specs=(whole, per_set), check_vma=False,
    )
```

time: 149 us -> 82.6 us (0.55)
  Pallas kernels: 143 us -> 78.7 us
  local copies, waits for them, and re-layouts: 4.98 us -> 2.93 us
    pallas_call x1, Pallas kernels: 143 us -> 78.7 us  [on_device(): pl.pallas_call(functools.partial(kernel, sizes), out_shape=(jax.ShapeDtyp...]
    unnamed x8 -> x4, local copies, waits for them, and re-layouts: 4.98 us -> 2.93 us
where the time goes in v2:
time: 82.6 us; the launch traced here: 82.2 us
  Pallas kernels  78.7 us (95%)
  local copies, waits for them, and re-layouts  2.93 us (4%)
    pallas_call x1, Pallas kernels, on_device(): pl.pallas_call(functools.partial(kernel, sizes), out_shape=(jax.ShapeDtyp...  78.7 us
    unnamed x4, local copies, waits for them, and re-layouts  2.93 us

profile of v2, /device:TPU:1, one launch (start us, length us, event | category | flops | bytes accessed | tf_op | source)
XLA Modules:
  0.0 82.2 jit_solution(14296338675640644409)
XLA Ops:
  0.6 78.7 %shard_map.68 = (f32[32,32,128]{2,1,0:T(8,128)}, f32[2,32,32,128]{3,2,1,0:T(8,128)}) custom-call(f32[32,32,128]{2,1,0:T(8,128)} %lr_hbm.1, f32[2,32,32,128]{3,2,1,0:T(8,128)} %st_hbm.1, f32[2,32,32,128]{3,2,1,0:T(8,128)} %x0_hbm.1, s32[2,1,4096]{2,1,0:T(1,128)} %bitcast.2, f32[2,1,4096]{2,1,0:T(1,128)} %bitcast.3), custom_call_target="tpu_custom_call" | custom-call | tf_op jit(solution)/shard_map/pallas_call | solution.py:477
  79.3 0.0 copy-start
  79.3 2.0 %copy.9 = f32[32,32,128]{2,1,0:T(8,128)} copy(f32[32,32,128]{2,1,0:T(8,128)} %get-tuple-element.4) | data formatting | bytes 1048576
  81.3 0.0 copy-done
  81.3 1.0 %copy.10 = f32[2,32,32,128]{3,2,1,0:T(8,128)} copy(f32[2,32,32,128]{3,2,1,0:T(8,128)S(1)} %copy-done) | data formatting | bytes 2097152
Async XLA Ops:
  79.3 2.0 %copy-start = (f32[2,32,32,128]{3,2,1,0:T(8,128)S(1)}, f32[2,32,32,128]{3,2,1,0:T(8,128)}, u32[]{:S(2)}) copy-start(f32[2,32,32,128]{3,2,1,0:T(8,128)} %get-tuple-element.5) | copy-start | bytes 3145732

commit v3 on v2

--- a/solution.py
+++ b/solution.py
@@ -12,19 +12,19 @@
 LANES = 128
 TOP = 8
 MESH = pl.DeviceIdType.MESH
-INTERIOR = 6
+INTERIOR = 10
 WHOLE = 8
 INV_NOISE = 4.0
 
 
 def kernel(
     sizes,
-    lr_hbm, st_hbm, x0_hbm, index_ref, value_ref,
+    lr_hbm, st_hbm, x0_hbm, index_hbm, value_hbm,
     grad_ref, adj_ref,
     kap, fp, ft, fs, part, xx, ax, pp, ap, ss, sa, rr, ra, zz, ww, bb, ast,
     ysp, yst, yss, zsp, zst, zss, yrp, yrt, yrs, zrp, zrt, zrs,
-    onehot_lo, onehot_hi, ar1, ar2, mine1, mine2,
-    send_sem, recv_sem, ar_send, ar_recv1, ar_recv2, local_sem,
+    onehot_lo, onehot_hi, index_ref, value_ref, rows_all, mine,
+    send_sem, recv_sem, sum_send, sum_recv, local_sem,
 ):
     gx_n, gy_n, gz_n = sizes
     nx, ny = kap.shape[0], kap.shape[1]
@@ -38,8 +38,13 @@
             lax.rem(gz + dz + gz_n, gz_n),
         )
 
-    plane = [(0, dy, dz) for dy in range(gy_n) for dz in range(gz_n) if (dy, dz) != (0, 0)]
-    column = [(dx, 0, 0) for dx in range(1, gx_n)]
+    def length(offset):
+        return sum(min(d, n - d) for d, n in zip(offset, sizes))
+
+    others = [
+        (dx, dy, dz) for dx in range(gx_n) for dy in range(gy_n) for dz in range(gz_n)
+    ][1:]
+    others.sort(key=length, reverse=True)
 
     inner = (slice(None), pl.ds(1, nx), pl.ds(TOP, ny), slice(None))
     loads = [
@@ -47,12 +52,14 @@
         pltpu.make_async_copy(st_hbm, fs.at[inner], local_sem.at[1]),
         pltpu.make_async_copy(lr_hbm, kap, local_sem.at[2]),
         pltpu.make_async_copy(x0_hbm, xx, local_sem.at[3]),
+        pltpu.make_async_copy(index_hbm, index_ref, local_sem.at[4]),
+        pltpu.make_async_copy(value_hbm, value_ref, local_sem.at[5]),
     ]
     for load in loads:
         load.start()
 
     barrier = pltpu.get_barrier_semaphore()
-    for offset in plane + column:
+    for offset in others:
         pl.semaphore_signal(barrier, inc=1, device_id=around(*offset), device_id_type=MESH)
 
     lane = lax.broadcasted_iota(jnp.int32, (8, LANES), 1)
@@ -193,100 +200,82 @@
     nobs = index_ref.shape[2]
     rows = onehot_hi.shape[0]
     step = 512
+    bf16 = jnp.bfloat16
     planes = rows // ny
+
+    halves = 2
+    rows_half = nx * ny // halves
+
+    def spread(count, numbers, weights):
+        hit = lax.broadcasted_iota(jnp.int32, (count, step), 0).astype(bf16) == numbers.astype(
+            jnp.float32
+        ).astype(bf16)
+        return [jnp.where(hit, weight, jnp.zeros_like(weight)) for weight in weights]
 
     def build(s):
         for k in range(0, nobs, step):
-            low = index_ref[s, :, k : k + step] % LANES
+            cell = index_ref[s, :, k : k + step]
+            low = cell % LANES + cell // (rows_half * LANES) * LANES
             v = value_ref[s, :, k : k + step]
-            v1 = v.astype(jnp.bfloat16).astype(jnp.float32)
-            v2 = (v - v1).astype(jnp.bfloat16).astype(jnp.float32)
-            v3 = v - v1 - v2
-            hit = lax.broadcasted_iota(jnp.int32, (LANES, step), 0) == low
-            for n, weight in enumerate((jnp.ones_like(v), v1, v2, v3)):
-                onehot_lo[LANES * n : LANES * (n + 1), k : k + step] = jnp.where(
-                    hit, weight, 0.0
-                ).astype(jnp.bfloat16)
+            v1 = v.astype(bf16)
+            v2 = (v - v1.astype(jnp.float32)).astype(bf16)
+            for n, tile in enumerate(spread(halves * LANES, low, (jnp.ones_like(v1), v1, v2))):
+                onehot_lo[halves * LANES * n : halves * LANES * (n + 1), k : k + step] = tile
 
     def observe(s, lo, hi):
         def body(m, _):
             for k in range(0, nobs, step):
-                high = index_ref[s, :, k : k + step] // LANES - m * rows
-                onehot_hi[:, k : k + step] = jnp.where(
-                    lax.broadcasted_iota(jnp.int32, (rows, step), 0) == high, 1.0, 0.0
-                ).astype(jnp.bfloat16)
+                high = index_ref[s, :, k : k + step] // LANES % rows_half
+                for r in range(0, rows, 256):
+                    ones = jnp.ones((1, step), bf16)
+                    onehot_hi[r : r + 256, k : k + step] = spread(256, high - (m * rows + r), (ones,))[0]
             sums = lax.dot_general(
                 onehot_hi[...], onehot_lo[...], (((1,), (1,)), ((), ())),
                 preferred_element_type=jnp.float32,
             )
-            count = sums[:, :LANES].reshape(planes, ny, LANES)
-            total = (sums[:, LANES : 2 * LANES] + sums[:, 2 * LANES : 3 * LANES]) + sums[:, 3 * LANES :]
-            total = total.reshape(planes, ny, LANES)
-            x = m * planes
-            ww[s, pl.ds(x, planes)] = INV_NOISE * count
-            bb[s, pl.ds(x, planes)] = INV_NOISE * (
-                total - count * fs[s, pl.ds(x + 1, planes), TOP : TOP + ny, :]
-            )
+            for h in range(halves):
+                count, high, low = (
+                    sums[:, (halves * n + h) * LANES : (halves * n + h + 1) * LANES] for n in range(3)
+                )
+                count = count.reshape(planes, ny, LANES)
+                total = (high + low).reshape(planes, ny, LANES)
+                x = h * (nx // halves) + m * planes
+                ww[s, pl.ds(x, planes)] = INV_NOISE * count
+                bb[s, pl.ds(x, planes)] = INV_NOISE * (
+                    total - count * fs[s, pl.ds(x + 1, planes), TOP : TOP + ny, :]
+                )
             return _
         sweep(body, 0, lo, hi)
 
-    me1 = gy * gz_n + gz
-    me2 = gx
+    me = (gx * gy_n + gy) * gz_n + gz
     lane_row = lax.broadcasted_iota(jnp.int32, (1, LANES), 1)
 
-    def first_stage(i, sums):
+    def begin_sums(i, sums):
         row = jnp.zeros((1, LANES), jnp.float32)
         for n, share in enumerate(sums):
             total = jnp.sum(jnp.sum(share, axis=0, keepdims=True), axis=1, keepdims=True)
             row = jnp.where(lane_row == n, total, row)
-        mine1[i] = row
-        ar1[i, me1] = row
-        copies = [
+        mine[i] = row
+        rows_all[i, me] = row
+        for offset in others:
             pltpu.make_async_remote_copy(
-                src_ref=mine1.at[i], dst_ref=ar1.at[i, me1], send_sem=ar_send.at[k],
-                recv_sem=ar_recv1.at[i, k], device_id=around(*offset), device_id_type=MESH,
-            )
-            for k, offset in enumerate(plane)
-        ]
-        for copy in copies:
-            copy.start()
-        return copies
-
-    def second_stage(i, copies):
-        for copy in copies:
-            copy.wait_recv()
-        row = jnp.sum(ar1[i], axis=0)
-        mine2[i] = row
-        ar2[i, me2] = row
-        later = [
-            pltpu.make_async_remote_copy(
-                src_ref=mine2.at[i], dst_ref=ar2.at[i, me2], send_sem=ar_send.at[len(plane) + k],
-                recv_sem=ar_recv2.at[i, k], device_id=around(*offset), device_id_type=MESH,
-            )
-            for k, offset in enumerate(column)
-        ]
-        for copy in later:
-            copy.start()
-        return copies + later
-
-    def last_stage(i, copies):
-        for copy in copies[len(plane) :]:
-            copy.wait_recv()
-        row = jnp.sum(ar2[i], axis=0)
-        for copy in copies:
-            copy.wait_send()
+                src_ref=mine.at[i], dst_ref=rows_all.at[i, me], send_sem=sum_send,
+                recv_sem=sum_recv.at[i], device_id=around(*offset), device_id_type=MESH,
+            ).start()
+
+    def end_sums(i):
+        every = rows_all.at[i, pl.ds(0, len(others))]
+        pltpu.make_async_copy(every, every, sum_recv.at[i]).wait()
+        row = jnp.sum(rows_all[i], axis=0)
+        pltpu.make_async_copy(every, every, sum_send).wait()
         return [
             jnp.sum(jnp.where(lane_row == n, row, 0.0), axis=1, keepdims=True) for n in range(2 * SETS)
         ]
 
-    sums_of = {}
     norm, size, alpha, beta = {}, {}, {}, {}
 
-    def middle(i):
-        sums_of[i] = second_stage(i, sums_of[i])
-
     def scalars(i):
-        totals = last_stage(i, sums_of[i])
+        totals = end_sums(i)
         norm[i], product = totals[:SETS], totals[SETS:]
         if i == 0:
             size[i] = [n / d for n, d in zip(norm[i], product)]
@@ -325,7 +314,7 @@
                     sums[s] = sums[s] + square
                     sums[SETS + s] = sums[SETS + s] + (r_image * r_image + ww[at] * square)
             return tuple(sums)
-        sums_of[i + 1] = first_stage(i + 1, sweep(body, (zero,) * (2 * SETS), 0, nx, 2))
+        begin_sums(i + 1, sweep(body, (zero,) * (2 * SETS), 0, nx, 2))
 
     no_faces = (zero,) * yb_n
 
@@ -345,20 +334,17 @@
     face_pass(fp, ysp, zsp)
     loads[2].wait()
     sweep(kappa, 0, 0, nx)
-    loads[1].wait()
-    face_pass(fs, yss, zss)
-    loads[3].wait()
+    for load in loads[1:2] + loads[3:]:
+        load.wait()
     build(0)
     observe(0, 0, 2)
-    pl.semaphore_wait(barrier, len(plane) + len(column))
+    pl.semaphore_wait(barrier, len(others))
     p_copies = faces(0, *p_kind)
     start(p_copies)
-    s_copies = faces(2, *s_kind)
-    start(s_copies)
 
     def gap():
-        observe(0, 2, 4)
         build(1)
+        observe(1, 0, 1)
 
     def emit_start(s, x, yb, out, acc):
         ft[s, x + 1, inner_rows(yb), :] = out
@@ -366,9 +352,12 @@
         return sent(yst, s, x, yb, out, acc)
 
     t_copies = send(1, t_kind, apply(fp, p_copies, yrp, zrp, emit_start, no_faces, gap))
+    s_copies = faces(2, *s_kind)
 
     def gap():
-        observe(1, 0, 4)
+        face_pass(fs, yss, zss)
+        start(s_copies)
+        observe(1, 1, 2)
 
     def emit_residual(s, x, yb, out, acc):
         at = (s, x, rows_of(yb), slice(None))
@@ -394,8 +383,8 @@
         return (sent(yst, s, x, yb, out, acc), tuple(sums))
 
     acc, sums = apply(fp, p_copies, yrp, zrp, emit_first, (no_faces, (zero,) * (2 * SETS)))
-    sums_of[0] = first_stage(0, sums)
     t_copies = send(1, t_kind, acc)
+    begin_sums(0, sums)
 
     def emit_image(s, x, yb, out, acc):
         at = (s, x, rows_of(yb), slice(None))
@@ -405,7 +394,7 @@
 
     acc = apply(
         ft, t_copies, yrt, zrt, emit_image, no_faces,
-        lambda: apply(fs, s_copies, yrs, zrs, emit_state, 0, part=ast), lambda: middle(0),
+        lambda: apply(fs, s_copies, yrs, zrs, emit_state, 0, part=ast),
     )
     p_copies = send(0, p_kind, acc)
 
@@ -428,10 +417,7 @@
             fp[s, x + 1, inner_rows(yb), :] = w
             return sent(ysp, s, x, yb, w, acc)
 
-        acc = apply(
-            fp, p_copies, yrp, zrp, emit_inner, no_faces, None,
-            None if i == 0 else functools.partial(middle, i),
-        )
+        acc = apply(fp, p_copies, yrp, zrp, emit_inner, no_faces)
         if last:
             advance(i)
         else:
@@ -442,7 +428,6 @@
             p_copies = send(0, p_kind, acc)
 
     i = ITERS - 1
-    middle(i)
     scalars(i)
 
     def finish(x, _):
@@ -470,9 +455,8 @@
     yface = pltpu.VMEM((2, SETS, nx, nz), f32)
     zsent = pltpu.VMEM((ny, LANES), f32)
     zgot = pltpu.VMEM((2, ny, LANES), f32)
-    group = sizes[1] * sizes[2]
     vmem = pl.BlockSpec(memory_space=pltpu.VMEM)
-    hbm = pl.BlockSpec(memory_space=pl.ANY)
+    hbm = pl.BlockSpec(memory_space=pltpu.HBM)
     dma = pltpu.SemaphoreType.DMA
     return pl.pallas_call(
         functools.partial(kernel, sizes),
@@ -480,23 +464,21 @@
             jax.ShapeDtypeStruct((nx, ny, nz), f32),
             jax.ShapeDtypeStruct((SETS, nx, ny, nz), f32),
         ),
-        in_specs=[hbm, hbm, hbm, vmem, vmem],
+        in_specs=[hbm] * 5,
         out_specs=(vmem, vmem),
         scratch_shapes=[
             pltpu.VMEM((nx, ny, nz), f32),
             padded, padded, padded,
             field, field, field, field, field, field, field, field, field, field, field, field, field,
             yface, yface, yface, zsent, zsent, zsent, yface, yface, yface, zgot, zgot, zgot,
-            pltpu.VMEM((4 * LANES, nobs), jnp.bfloat16),
+            pltpu.VMEM((6 * LANES, nobs), jnp.bfloat16),
             pltpu.VMEM((256, nobs), jnp.bfloat16),
-            pltpu.VMEM((ITERS, group, 1, LANES), f32),
-            pltpu.VMEM((ITERS, sizes[0], 1, LANES), f32),
+            pltpu.VMEM((SETS, 1, nobs), jnp.int32),
+            pltpu.VMEM((SETS, 1, nobs), f32),
+            pltpu.VMEM((ITERS, sizes[0] * sizes[1] * sizes[2], 1, LANES), f32),
             pltpu.VMEM((ITERS, 1, LANES), f32),
-            pltpu.VMEM((ITERS, 1, LANES), f32),
-            dma((3, 6)), dma((3, 6)),
-            dma((group + sizes[0] - 2,)),
-            dma((ITERS, group - 1)), dma((ITERS, sizes[0] - 1)),
-            dma((4,)),
+            dma((3, 6)), dma((3, 6)), dma, dma((ITERS,)),
+            dma((6,)),
         ],
         compiler_params=pltpu.CompilerParams(
             collective_id=0, has_side_effects=True, vmem_limit_bytes=60 * 1024 * 1024

time: 82.6 us -> 71.6 us (0.87)
  Pallas kernels: 78.7 us -> 67.9 us
    pallas_call x1, Pallas kernels: 78.7 us -> 67.9 us  [on_device(): pl.pallas_call(functools.partial(kernel, sizes), out_shape=(jax.ShapeDtyp...]
where the time goes in v3:
time: 71.6 us; the launch traced here: 71.5 us
  Pallas kernels  67.9 us (95%)
  local copies, waits for them, and re-layouts  2.93 us (4%)
    pallas_call x1, Pallas kernels, on_device(): pl.pallas_call(functools.partial(kernel, sizes), out_shape=(jax.ShapeDtyp...  67.9 us
    unnamed x4, local copies, waits for them, and re-layouts  2.93 us

profile of v3, /device:TPU:1, one launch (start us, length us, event | category | flops | bytes accessed | tf_op | source)
XLA Modules:
  0.0 71.5 jit_solution(11967965044336749102)
XLA Ops:
  0.6 67.9 %shard_map.68 = (f32[32,32,128]{2,1,0:T(8,128)}, f32[2,32,32,128]{3,2,1,0:T(8,128)}) custom-call(f32[32,32,128]{2,1,0:T(8,128)} %lr_hbm.1, f32[2,32,32,128]{3,2,1,0:T(8,128)} %st_hbm.1, f32[2,32,32,128]{3,2,1,0:T(8,128)} %x0_hbm.1, s32[2,1,4096]{2,1,0:T(1,128)} %bitcast.2, f32[2,1,4096]{2,1,0:T(1,128)} %bitcast.3), custom_call_target="tpu_custom_call" | custom-call | tf_op jit(solution)/shard_map/pallas_call | solution.py:461
  68.5 0.0 copy-start
  68.5 2.0 %copy.9 = f32[32,32,128]{2,1,0:T(8,128)} copy(f32[32,32,128]{2,1,0:T(8,128)} %get-tuple-element.4) | data formatting | bytes 1048576
  70.5 0.0 copy-done
  70.5 1.0 %copy.10 = f32[2,32,32,128]{3,2,1,0:T(8,128)} copy(f32[2,32,32,128]{3,2,1,0:T(8,128)S(1)} %copy-done) | data formatting | bytes 2097152
Async XLA Ops:
  68.5 2.0 %copy-start = (f32[2,32,32,128]{3,2,1,0:T(8,128)S(1)}, f32[2,32,32,128]{3,2,1,0:T(8,128)}, u32[]{:S(2)}) copy-start(f32[2,32,32,128]{3,2,1,0:T(8,128)} %get-tuple-element.5) | copy-start | bytes 3145732

commit v4 on v3

--- a/solution.py
+++ b/solution.py
@@ -12,8 +12,8 @@
 LANES = 128
 TOP = 8
 MESH = pl.DeviceIdType.MESH
-INTERIOR = 10
-WHOLE = 8
+INTERIOR = 15
+WHOLE = 16
 INV_NOISE = 4.0
 
 
@@ -21,10 +21,10 @@
     sizes,
     lr_hbm, st_hbm, x0_hbm, index_hbm, value_hbm,
     grad_ref, adj_ref,
-    kap, fp, ft, fs, part, xx, ax, pp, ap, ss, sa, rr, ra, zz, ww, bb, ast,
+    kap, fp, ft, fs, part, xx, ax, pp, ap, ss, sa, rr, ra, rs, rt, zz, ww, bb, ast,
     ysp, yst, yss, zsp, zst, zss, yrp, yrt, yrs, zrp, zrt, zrs,
-    onehot_lo, onehot_hi, index_ref, value_ref, rows_all, mine,
-    send_sem, recv_sem, sum_send, sum_recv, local_sem,
+    onehot_lo, onehot_hi, index_ref, value_ref, rows_all, rows_near, mine, ours,
+    send_sem, recv_sem, sum_send, sum_recv, local_sem, out_sem,
 ):
     gx_n, gy_n, gz_n = sizes
     nx, ny = kap.shape[0], kap.shape[1]
@@ -250,24 +250,52 @@
     me = (gx * gy_n + gy) * gz_n + gz
     lane_row = lax.broadcasted_iota(jnp.int32, (1, LANES), 1)
 
+    def row_copies(i, source, to, slot, sent, got, offsets):
+        for offset in offsets:
+            pltpu.make_async_remote_copy(
+                src_ref=source.at[i], dst_ref=to.at[i, slot], send_sem=sent,
+                recv_sem=got, device_id=around(*offset), device_id_type=MESH,
+            ).start()
+
+    def wait_rows(i, rows, count, sem):
+        every = rows.at[i, pl.ds(0, count)]
+        pltpu.make_async_copy(every, every, sem).wait()
+
+    near = [(0, 0, dz) for dz in range(1, gz_n)]
+    far = [offset for offset in others if offset[2] == 0]
+    direct = ITERS - 1
+
     def begin_sums(i, sums):
         row = jnp.zeros((1, LANES), jnp.float32)
         for n, share in enumerate(sums):
             total = jnp.sum(jnp.sum(share, axis=0, keepdims=True), axis=1, keepdims=True)
             row = jnp.where(lane_row == n, total, row)
         mine[i] = row
-        rows_all[i, me] = row
-        for offset in others:
-            pltpu.make_async_remote_copy(
-                src_ref=mine.at[i], dst_ref=rows_all.at[i, me], send_sem=sum_send,
-                recv_sem=sum_recv.at[i], device_id=around(*offset), device_id_type=MESH,
-            ).start()
+        if i == direct:
+            rows_all[i, me] = row
+            row_copies(i, mine, rows_all, me, sum_send.at[0], sum_recv.at[i, 0], others)
+        else:
+            rows_near[i, gz] = row
+            row_copies(i, mine, rows_near, gz, sum_send.at[0], sum_recv.at[i, 0], near)
+
+    def forward_sums(i):
+        wait_rows(i, rows_near, len(near), sum_recv.at[i, 0])
+        row = jnp.sum(rows_near[i], axis=0)
+        group = gx * gy_n + gy
+        ours[i] = row
+        rows_all[i, group] = row
+        row_copies(i, ours, rows_all, group, sum_send.at[1], sum_recv.at[i, 1], far)
 
     def end_sums(i):
-        every = rows_all.at[i, pl.ds(0, len(others))]
-        pltpu.make_async_copy(every, every, sum_recv.at[i]).wait()
-        row = jnp.sum(rows_all[i], axis=0)
-        pltpu.make_async_copy(every, every, sum_send).wait()
+        if i == direct:
+            wait_rows(i, rows_all, len(others), sum_recv.at[i, 0])
+            row = jnp.sum(rows_all[i], axis=0)
+            wait_rows(i, rows_all, len(others), sum_send.at[0])
+        else:
+            wait_rows(i, rows_all, len(far), sum_recv.at[i, 1])
+            row = jnp.sum(rows_all[i, 0 : gx_n * gy_n], axis=0)
+            wait_rows(i, rows_near, len(near), sum_send.at[0])
+            wait_rows(i, rows_all, len(far), sum_send.at[1])
         return [
             jnp.sum(jnp.where(lane_row == n, row, 0.0), axis=1, keepdims=True) for n in range(2 * SETS)
         ]
@@ -293,28 +321,38 @@
             for s in range(SETS):
                 for yb in range(yb_n):
                     at = (s, x, rows_of(yb), slice(None))
-                    r, r_image = rr[at], ra[at]
-                    p, p_image = r, r_image
                     q = fp[s, x + 1, inner_rows(yb), :]
                     q_image = ft[s, x + 1, inner_rows(yb), :]
                     if i > 0:
-                        p = p + beta[i][s] * pp[at]
-                        p_image = p_image + beta[i][s] * ap[at]
                         q = q + beta[i][s] * ss[at]
                         q_image = q_image + beta[i][s] * sa[at]
-                    pp[at], ap[at] = p, p_image
                     if i + 2 < ITERS:
                         ss[at], sa[at] = q, q_image
-                    xx[at] += alpha[i][s] * p
-                    ax[at] += alpha[i][s] * p_image
-                    r = r - alpha[i][s] * q
-                    r_image = r_image - alpha[i][s] * q_image
-                    rr[at], ra[at] = r, r_image
+                    fresh, fresh_image = (rr, ra) if i % 2 else (rs, rt)
+                    old, old_image = (rs, rt) if i % 2 else (rr, ra)
+                    r = old[at] - alpha[i][s] * q
+                    r_image = old_image[at] - alpha[i][s] * q_image
+                    fresh[at], fresh_image[at] = r, r_image
                     square = r * r
                     sums[s] = sums[s] + square
                     sums[SETS + s] = sums[SETS + s] + (r_image * r_image + ww[at] * square)
             return tuple(sums)
-        begin_sums(i + 1, sweep(body, (zero,) * (2 * SETS), 0, nx, 2))
+        begin_sums(i + 1, sweep(body, (zero,) * (2 * SETS), 0, nx, 4))
+
+        def settle(x, _):
+            old, old_image = (rs, rt) if i % 2 else (rr, ra)
+            for s in range(SETS):
+                for yb in range(yb_n):
+                    at = (s, x, rows_of(yb), slice(None))
+                    p, p_image = old[at], old_image[at]
+                    if i > 0:
+                        p = p + beta[i][s] * pp[at]
+                        p_image = p_image + beta[i][s] * ap[at]
+                    pp[at], ap[at] = p, p_image
+                    xx[at] += alpha[i][s] * p
+                    ax[at] += alpha[i][s] * p_image
+            return _
+        sweep(settle, 0, 0, nx, 4)
 
     no_faces = (zero,) * yb_n
 
@@ -344,7 +382,7 @@
 
     def gap():
         build(1)
-        observe(1, 0, 1)
+        observe(1, 0, 2)
 
     def emit_start(s, x, yb, out, acc):
         ft[s, x + 1, inner_rows(yb), :] = out
@@ -357,7 +395,6 @@
     def gap():
         face_pass(fs, yss, zss)
         start(s_copies)
-        observe(1, 1, 2)
 
     def emit_residual(s, x, yb, out, acc):
         at = (s, x, rows_of(yb), slice(None))
@@ -394,7 +431,7 @@
 
     acc = apply(
         ft, t_copies, yrt, zrt, emit_image, no_faces,
-        lambda: apply(fs, s_copies, yrs, zrs, emit_state, 0, part=ast),
+        lambda: apply(fs, s_copies, yrs, zrs, emit_state, 0, part=ast), lambda: forward_sums(0),
     )
     p_copies = send(0, p_kind, acc)
 
@@ -423,27 +460,81 @@
         else:
             t_copies = send(1, t_kind, acc)
             acc = apply(
-                ft, t_copies, yrt, zrt, emit_outer, no_faces, functools.partial(advance, i)
+                ft, t_copies, yrt, zrt, emit_outer, no_faces, functools.partial(advance, i),
+                functools.partial(forward_sums, i + 1),
             )
             p_copies = send(0, p_kind, acc)
 
     i = ITERS - 1
     scalars(i)
+
+    final, final_image = (rr, ra) if (ITERS - 2) % 2 else (rs, rt)
 
     def finish(x, _):
         for yb in range(yb_n):
             total = zero
             for s in range(SETS):
                 at = (s, x, rows_of(yb), slice(None))
-                p = rr[at] + beta[i][s] * pp[at]
-                p_image = ra[at] + beta[i][s] * ap[at]
+                p = final[at] + beta[i][s] * pp[at]
+                p_image = final_image[at] + beta[i][s] * ap[at]
                 adjoint = xx[at] + alpha[i][s] * p
                 image = ax[at] + alpha[i][s] * p_image
-                adj_ref[at] = adjoint
+                xx[at] = adjoint
                 total = total + (adjoint * ast[at] + image * fs[s, x + 1, inner_rows(yb), :])
-            grad_ref[x, rows_of(yb), :] = -2.0 * kap[x, rows_of(yb), :] * total
+            kap[x, rows_of(yb), :] = -2.0 * kap[x, rows_of(yb), :] * total
         return _
-    sweep(finish, 0, 0, nx, 2)
+
+    stores = []
+    share = nx // 4
+    for n in range(4):
+        sweep(finish, 0, n * share, (n + 1) * share, 2)
+        at = pl.ds(n * share, share)
+        stores.append(pltpu.make_async_copy(xx.at[:, at], adj_ref.at[:, at], out_sem.at[n, 0]))
+        stores.append(pltpu.make_async_copy(kap.at[at], grad_ref.at[at], out_sem.at[n, 1]))
+        stores[-2].start()
+        stores[-1].start()
+    for store in stores:
+        store.wait()
+
+
+def hand_over(gradient, adjoint):
+    nx, ny, nz = gradient.shape
+    share = nx // 4
+
+    def body(gradient_hbm, adjoint_hbm, gradient_out, adjoint_out, gradient_buf, adjoint_buf, got, put):
+        reads, writes = [], []
+        for n in range(4):
+            at = pl.ds(n * share, share)
+            reads += [
+                pltpu.make_async_copy(gradient_hbm.at[at], gradient_buf.at[at], got.at[n, 0]),
+                pltpu.make_async_copy(adjoint_hbm.at[:, at], adjoint_buf.at[:, at], got.at[n, 1]),
+            ]
+            writes += [
+                pltpu.make_async_copy(gradient_buf.at[at], gradient_out.at[at], put.at[n, 0]),
+                pltpu.make_async_copy(adjoint_buf.at[:, at], adjoint_out.at[:, at], put.at[n, 1]),
+            ]
+        for read in reads:
+            read.start()
+        for read, write in zip(reads, writes):
+            read.wait()
+            write.start()
+        for write in writes:
+            write.wait()
+
+    hbm = pl.BlockSpec(memory_space=pl.ANY)
+    return pl.pallas_call(
+        body,
+        out_shape=(
+            jax.ShapeDtypeStruct(gradient.shape, gradient.dtype),
+            jax.ShapeDtypeStruct(adjoint.shape, adjoint.dtype),
+        ),
+        in_specs=[hbm, hbm], out_specs=(hbm, hbm),
+        scratch_shapes=[
+            pltpu.VMEM(gradient.shape, gradient.dtype), pltpu.VMEM(adjoint.shape, adjoint.dtype),
+            pltpu.SemaphoreType.DMA((4, 2)), pltpu.SemaphoreType.DMA((4, 2)),
+        ],
+        compiler_params=pltpu.CompilerParams(vmem_limit_bytes=60 * 1024 * 1024),
+    )(gradient, adjoint)
 
 
 def on_device(sizes, log_range, state, adjoint_start, obs_index, obs_value):
@@ -455,20 +546,19 @@
     yface = pltpu.VMEM((2, SETS, nx, nz), f32)
     zsent = pltpu.VMEM((ny, LANES), f32)
     zgot = pltpu.VMEM((2, ny, LANES), f32)
-    vmem = pl.BlockSpec(memory_space=pltpu.VMEM)
-    hbm = pl.BlockSpec(memory_space=pltpu.HBM)
+    hbm = pl.BlockSpec(memory_space=pl.ANY)
     dma = pltpu.SemaphoreType.DMA
-    return pl.pallas_call(
+    gradient, adjoint = pl.pallas_call(
         functools.partial(kernel, sizes),
         out_shape=(
             jax.ShapeDtypeStruct((nx, ny, nz), f32),
             jax.ShapeDtypeStruct((SETS, nx, ny, nz), f32),
         ),
         in_specs=[hbm] * 5,
-        out_specs=(vmem, vmem),
+        out_specs=(hbm, hbm),
         scratch_shapes=[
             pltpu.VMEM((nx, ny, nz), f32),
-            padded, padded, padded,
+            padded, padded, padded, field, field,
             field, field, field, field, field, field, field, field, field, field, field, field, field,
             yface, yface, yface, zsent, zsent, zsent, yface, yface, yface, zgot, zgot, zgot,
             pltpu.VMEM((6 * LANES, nobs), jnp.bfloat16),
@@ -476,9 +566,11 @@
             pltpu.VMEM((SETS, 1, nobs), jnp.int32),
             pltpu.VMEM((SETS, 1, nobs), f32),
             pltpu.VMEM((ITERS, sizes[0] * sizes[1] * sizes[2], 1, LANES), f32),
+            pltpu.VMEM((ITERS, sizes[2], 1, LANES), f32),
             pltpu.VMEM((ITERS, 1, LANES), f32),
-            dma((3, 6)), dma((3, 6)), dma, dma((ITERS,)),
-            dma((6,)),
+            pltpu.VMEM((ITERS, 1, LANES), f32),
+            dma((3, 6)), dma((3, 6)), dma((2,)), dma((ITERS, 2)),
+            dma((6,)), dma((4, 2)),
         ],
         compiler_params=pltpu.CompilerParams(
             collective_id=0, has_side_effects=True, vmem_limit_bytes=60 * 1024 * 1024
@@ -487,6 +579,7 @@
         log_range, state, adjoint_start,
         obs_index.reshape(SETS, 1, nobs), obs_value.reshape(SETS, 1, nobs),
     )
+    return hand_over(gradient, adjoint)
 
 
 def solution(mesh):

time: 71.6 us -> 69.9 us (0.976)
  local copies, waits for them, and re-layouts: 2.93 us -> 0 us
  Pallas kernels: 67.9 us -> 68.9 us
    unnamed x4 -> x0, local copies, waits for them, and re-layouts: 2.93 us -> none
    pallas_call x0 -> x1, Pallas kernels: none -> 2.26 us  [hand_over(): pl.pallas_call(body, out_shape=(jax.ShapeDtypeStruct(gradient.shape, grad...]
    pallas_call x1, Pallas kernels: 67.9 us -> 66.7 us  [on_device(): pl.pallas_call(functools.partial(kernel, sizes), out_shape=(jax.ShapeDtyp...]
where the time goes in v4:
time: 69.9 us; the launch traced here: 69.7 us
  Pallas kernels  68.9 us (99%)
  between operations  0.8 us (1%)
    pallas_call x1, Pallas kernels, on_device(): pl.pallas_call(functools.partial(kernel, sizes), out_shape=(jax.ShapeDtyp...  66.7 us
    pallas_call x1, Pallas kernels, hand_over(): pl.pallas_call(body, out_shape=(jax.ShapeDtypeStruct(gradient.shape, grad...  2.26 us

profile of v4, /device:TPU:1, one launch (start us, length us, event | category | flops | bytes accessed | tf_op | source)
XLA Modules:
  0.0 69.7 jit_solution(6664913804285421450)
XLA Ops:
  0.6 66.7 %shard_map.68 = (f32[32,32,128]{2,1,0:T(8,128)}, f32[2,32,32,128]{3,2,1,0:T(8,128)}) custom-call(f32[32,32,128]{2,1,0:T(8,128)} %lr_hbm.1, f32[2,32,32,128]{3,2,1,0:T(8,128)} %st_hbm.1, f32[2,32,32,128]{3,2,1,0:T(8,128)} %x0_hbm.1, s32[2,1,4096]{2,1,0:T(1,128)} %bitcast.2, f32[2,1,4096]{2,1,0:T(1,128)} %bitcast.3), custom_call_target="tpu_custom_call" | custom-call | tf_op jit(solution)/shard_map/pallas_call | solution.py:551
  67.3 2.3 %shard_map.69 = (f32[32,32,128]{2,1,0:T(8,128)}, f32[2,32,32,128]{3,2,1,0:T(8,128)}) custom-call(f32[32,32,128]{2,1,0:T(8,128)} %get-tuple-element.4.gradient_hbm, f32[2,32,32,128]{3,2,1,0:T(8,128)} %get-tuple-element.5.adjoint_hbm), custom_call_target="tpu_custom_call" | custom-call | tf_op jit(solution)/shard_map/pallas_call | solution.py:525

commit v5 on v4

--- a/solution.py
+++ b/solution.py
@@ -263,7 +263,7 @@
 
     near = [(0, 0, dz) for dz in range(1, gz_n)]
     far = [offset for offset in others if offset[2] == 0]
-    direct = ITERS - 1
+    direct = ITERS - 2
 
     def begin_sums(i, sums):
         row = jnp.zeros((1, LANES), jnp.float32)
@@ -271,7 +271,7 @@
             total = jnp.sum(jnp.sum(share, axis=0, keepdims=True), axis=1, keepdims=True)
             row = jnp.where(lane_row == n, total, row)
         mine[i] = row
-        if i == direct:
+        if i >= direct:
             rows_all[i, me] = row
             row_copies(i, mine, rows_all, me, sum_send.at[0], sum_recv.at[i, 0], others)
         else:
@@ -287,7 +287,7 @@
         row_copies(i, ours, rows_all, group, sum_send.at[1], sum_recv.at[i, 1], far)
 
     def end_sums(i):
-        if i == direct:
+        if i >= direct:
             wait_rows(i, rows_all, len(others), sum_recv.at[i, 0])
             row = jnp.sum(rows_all[i], axis=0)
             wait_rows(i, rows_all, len(others), sum_send.at[0])
@@ -431,9 +431,10 @@
 
     acc = apply(
         ft, t_copies, yrt, zrt, emit_image, no_faces,
-        lambda: apply(fs, s_copies, yrs, zrs, emit_state, 0, part=ast), lambda: forward_sums(0),
+        lambda: apply(fs, s_copies, yrs, zrs, emit_state, 0, part=ast),
     )
     p_copies = send(0, p_kind, acc)
+    forward_sums(0)
 
     for i in range(ITERS - 1):
         last = i + 2 == ITERS
@@ -460,10 +461,11 @@
         else:
             t_copies = send(1, t_kind, acc)
             acc = apply(
-                ft, t_copies, yrt, zrt, emit_outer, no_faces, functools.partial(advance, i),
-                functools.partial(forward_sums, i + 1),
+                ft, t_copies, yrt, zrt, emit_outer, no_faces, functools.partial(advance, i)
             )
             p_copies = send(0, p_kind, acc)
+            if i + 1 < direct:
+                forward_sums(i + 1)
 
     i = ITERS - 1
     scalars(i)

time: 69.9 us -> 69.9 us (level)
  no operation moved by 1% of the time
where the time goes in v5:
time: 69.9 us; the launch traced here: 69.7 us
  Pallas kernels  68.9 us (99%)
  between operations  0.8 us (1%)
    pallas_call x1, Pallas kernels, on_device(): pl.pallas_call(functools.partial(kernel, sizes), out_shape=(jax.ShapeDtyp...  66.7 us
    pallas_call x1, Pallas kernels, hand_over(): pl.pallas_call(body, out_shape=(jax.ShapeDtypeStruct(gradient.shape, grad...  2.26 us

profile of v5, /device:TPU:1, one launch (start us, length us, event | category | flops | bytes accessed | tf_op | source)
XLA Modules:
  0.0 69.7 jit_solution(13040189227757646195)
XLA Ops:
  0.6 66.7 %shard_map.68 = (f32[32,32,128]{2,1,0:T(8,128)}, f32[2,32,32,128]{3,2,1,0:T(8,128)}) custom-call(f32[32,32,128]{2,1,0:T(8,128)} %lr_hbm.1, f32[2,32,32,128]{3,2,1,0:T(8,128)} %st_hbm.1, f32[2,32,32,128]{3,2,1,0:T(8,128)} %x0_hbm.1, s32[2,1,4096]{2,1,0:T(1,128)} %bitcast.2, f32[2,1,4096]{2,1,0:T(1,128)} %bitcast.3), custom_call_target="tpu_custom_call" | custom-call | tf_op jit(solution)/shard_map/pallas_call | solution.py:553
  67.3 2.3 %shard_map.69 = (f32[32,32,128]{2,1,0:T(8,128)}, f32[2,32,32,128]{3,2,1,0:T(8,128)}) custom-call(f32[32,32,128]{2,1,0:T(8,128)} %get-tuple-element.4.gradient_hbm, f32[2,32,32,128]{3,2,1,0:T(8,128)} %get-tuple-element.5.adjoint_hbm), custom_call_target="tpu_custom_call" | custom-call | tf_op jit(solution)/shard_map/pallas_call | solution.py:527
